TPU v7x, 32 devices: a whole 2x2x4 slice. The times are simulated.
32 devices in a mesh: cfg: 2 (over x), ta: 16 (over z, y, core).
Axes of the slice: x: 2, y: 2, z: 4, core: 2. Of those that a mesh axis runs over, the one named last changes fastest.
Arguments:
- fine_source: bfloat16 [32, 128, 2, 2, 24, 128], P('cfg', 'ta'), parts along dimension 0, may hold values from -24 to 24
- projectors: bfloat16 [32, 128, 2304], P(('cfg', 'ta')), parts along dimension 0, may hold values from -0.21875 to 0.21875
- stencil_links: bfloat16 [32, 8, 48, 864], P(('cfg', 'ta')), parts along dimension 0, may hold values from -0.21875 to 0.21875
- quark_mass: float32 [2], P('cfg'), parts along dimension 0, may hold values from 1.5 to 3
Outputs:
- solution: float32 [32, 8, 96, 128], P(('cfg', 'ta')), parts along dimension 0
- residual: float32 [32, 8, 96, 128], P(('cfg', 'ta')), parts along dimension 0
There are 2 independent parts, one for each index of `cfg`. A program takes and returns all parts, laid end to end along the dimension named above; each array names one. Nothing has to cross between parts.
All inputs are finite; a program needn't handle non-finite values.
Results may differ from a plain program's by a relative error of at most 0.012.
The roundings to bfloat16 on the way count: a program that leaves them out, or rounds other values in their place, can miss the bound.
Values may be sent and summed in bfloat16 or wider, within the bound.
No kernel may reach another device: no remote copies, remote signals or barrier semaphores. Data moves between devices by JAX's collectives and lax.ppermute only.
A program may use at most 128 MiB of HBM per device.

v0:
```python
import math

import jax
import jax.numpy as jnp
from jax import lax
from jax.sharding import PartitionSpec as P

LX = 4
LZ = 8
ITERS = 3


def from_behind(value, axis, steps):
    count = lax.axis_size(axis)
    pairs = [(source, (source + steps) % count) for source in range(count)]
    return lax.ppermute(value, axis, pairs)


def real_weights(proj_view):
    proj_re = proj_view[..., 0, :]
    proj_im = proj_view[..., 1, :]
    first_row = jnp.stack([proj_re, proj_im], axis=-4)
    second_row = jnp.stack([-proj_im, proj_re], axis=-4)
    return jnp.stack([first_row, second_row], axis=-5)


def inner_local(left, right, comp_count):
    left_re = left[:, :comp_count]
    left_im = left[:, comp_count:]
    right_re = right[:, :comp_count]
    right_im = right[:, comp_count:]
    return (
        jnp.sum(left_re * right_re + left_im * right_im, axis=(0, 1)),
        jnp.sum(left_re * right_im - left_im * right_re, axis=(0, 1)),
    )


def scaled(vector, factor_re, factor_im, comp_count):
    vector_re = vector[:, :comp_count]
    vector_im = vector[:, comp_count:]
    return jnp.concatenate(
        [
            factor_re * vector_re - factor_im * vector_im,
            factor_re * vector_im + factor_im * vector_re,
        ],
        axis=1,
    )


def shards(fine_source, projectors, stencil_links, quark_mass):
    comp_count = stencil_links.shape[2]
    null_count = comp_count // 2
    site_count = stencil_links.shape[1]
    column_count = projectors.shape[1]
    block_count = column_count // site_count
    fine_count = fine_source.shape[4]
    rhs_count = fine_source.shape[5]
    plane_count = fine_source.shape[0]
    moved_proj = lax.all_to_all(projectors, "ta", split_axis=1, concat_axis=0, tiled=True)
    local_columns = fine_source.shape[1]
    group_size = math.gcd(block_count, local_columns)
    groups = local_columns // group_size
    weights = real_weights(
        moved_proj.reshape(plane_count, groups, group_size, 2, null_count, 2, fine_count)
    )
    fine_local = fine_source.reshape(plane_count, groups, group_size, 2, 2, fine_count, rhs_count)
    partial_sums = jnp.einsum(
        "pmgdchvk,pmgchkr->pmdhvr", weights, fine_local, preferred_element_type=jnp.float32
    )
    partial_sums = partial_sums.reshape(plane_count, groups, 2 * comp_count, rhs_count)
    collected = lax.all_to_all(partial_sums, "ta", split_axis=0, concat_axis=1, tiled=True)
    source = jnp.sum(
        collected.reshape(site_count, block_count // group_size, 2 * comp_count, rhs_count), axis=1
    )
    link_view = stencil_links.reshape(site_count, comp_count, 9, 2, comp_count)
    link_re = link_view[:, :, :, 0, :]
    link_im = link_view[:, :, :, 1, :]
    upper_rows = jnp.stack([link_re, -link_im], axis=3)
    lower_rows = jnp.stack([link_im, link_re], axis=3)
    real_operator = jnp.stack([upper_rows, lower_rows], axis=1).reshape(
        site_count, 2 * comp_count, 18 * comp_count
    )
    mass_value = quark_mass[0]
    z_position = lax.axis_index("ta") % LZ
    line_count = site_count // LX

    def flatten_sites(shifted):
        return shifted.reshape(site_count, 2 * comp_count, rhs_count)

    solution = jnp.zeros_like(source)
    residual = source
    basis_q = []
    basis_p = []
    for iteration in range(ITERS):
        direction = residual
        rounded = residual.astype(jnp.bfloat16)
        plane_view = rounded.reshape(line_count, LX, 2 * comp_count, rhs_count)
        x_plus = flatten_sites(jnp.roll(plane_view, -1, axis=1))
        x_minus = flatten_sites(jnp.roll(plane_view, 1, axis=1))
        y_plus = flatten_sites(jnp.roll(plane_view, -1, axis=0))
        y_minus = flatten_sites(jnp.roll(plane_view, 1, axis=0))
        z_plus_near = from_behind(rounded, "ta", -1)
        z_minus_near = from_behind(rounded, "ta", 1)
        upper_pair = from_behind(jnp.stack([rounded, z_minus_near], axis=0), "ta", -LZ)
        lower_pair = from_behind(jnp.stack([rounded, z_plus_near], axis=0), "ta", LZ)
        t_plus = upper_pair[0]
        t_minus = lower_pair[0]
        z_plus = jnp.where(z_position == LZ - 1, lower_pair[1], z_plus_near)
        z_minus = jnp.where(z_position == 0, upper_pair[1], z_minus_near)
        stacked = jnp.stack(
            [rounded, x_plus, x_minus, y_plus, y_minus, z_plus, z_minus, t_plus, t_minus], axis=1
        )
        stacked = stacked.reshape(site_count, 18 * comp_count, rhs_count)
        product = jnp.einsum(
            "sij,sjr->sir", real_operator, stacked, preferred_element_type=jnp.float32
        )
        mapped = product + mass_value * rounded.astype(jnp.float32)
        square_loc = inner_local(mapped, mapped, comp_count)[0]
        cross_re, cross_im = inner_local(mapped, residual, comp_count)
        if iteration > 0:
            coef_pairs = [inner_local(earlier, mapped, comp_count) for earlier in basis_q]
            back_pairs = [inner_local(earlier, residual, comp_count) for earlier in basis_q]
            coef_re = jnp.stack([pair[0] for pair in coef_pairs])
            coef_im = jnp.stack([pair[1] for pair in coef_pairs])
            back_re = jnp.stack([pair[0] for pair in back_pairs])
            back_im = jnp.stack([pair[1] for pair in back_pairs])
        else:
            coef_re = jnp.zeros((1, rhs_count), jnp.float32)
            coef_im = jnp.zeros((1, rhs_count), jnp.float32)
            back_re = jnp.zeros((1, rhs_count), jnp.float32)
            back_im = jnp.zeros((1, rhs_count), jnp.float32)
        square_all, cross_re, cross_im, coef_re, coef_im, back_re, back_im = lax.psum(
            (square_loc, cross_re, cross_im, coef_re, coef_im, back_re, back_im), "ta"
        )
        squared = square_all
        proj_re = cross_re
        proj_im = cross_im
        for number in range(iteration):
            mapped = mapped - scaled(basis_q[number], coef_re[number], coef_im[number], comp_count)
            direction = direction - scaled(
                basis_p[number], coef_re[number], coef_im[number], comp_count
            )
            squared = squared - (
                coef_re[number] * coef_re[number] + coef_im[number] * coef_im[number]
            )
            proj_re = proj_re - (
                coef_re[number] * back_re[number] + coef_im[number] * back_im[number]
            )
            proj_im = proj_im - (
                coef_re[number] * back_im[number] - coef_im[number] * back_re[number]
            )
        factor = 1.0 / jnp.sqrt(squared + 1e-06)
        unit_q = mapped * factor
        unit_p = direction * factor
        alpha_re = proj_re * factor
        alpha_im = proj_im * factor
        solution = solution + scaled(unit_p, alpha_re, alpha_im, comp_count)
        residual = residual - scaled(unit_q, alpha_re, alpha_im, comp_count)
        basis_q.append(unit_q)
        basis_p.append(unit_p)
    return (
        solution.reshape(1, site_count, 2 * comp_count, rhs_count),
        residual.reshape(1, site_count, 2 * comp_count, rhs_count),
    )


def solution(mesh):
    return jax.shard_map(
        shards,
        mesh=mesh,
        in_specs=(
            P("cfg", "ta", None, None, None, None),
            P(("cfg", "ta"), None, None),
            P(("cfg", "ta"), None, None, None),
            P("cfg"),
        ),
        out_specs=(P(("cfg", "ta"), None, None, None), P(("cfg", "ta"), None, None, None)),
        check_vma=False,
    )
```

profile of v0, /device:TPU:0, one launch (start us, length us, event | category | flops | bytes accessed | tf_op | source)
XLA Modules:
  0.0 329.3 jit_solution(6759608211472331523)
XLA Ops:
  4.3 6.0 %reduce.2 = bf16[128,2304]{1,0:T(8,128)(2,1)} reduce(bf16[128,1,2304]{2,1,0:T(2,128)(2,1)} %bitcast.350, bf16[]{:T(256)} %broadcast.28), dimensions={1}, to_apply=%bitcast.316.reduce_sub_computation | reduce | bytes 1179650
  12.9 7.6 %all-to-all-start = ((bf16[16,2,9216]{2,1,0:T(2,128)(2,1)}), bf16[16,2,9216]{2,1,0:T(2,128)(2,1)}, u32[]{:S(2)}, u32[]{:S(2)}) async-start(bf16[16,2,9216]{2,1,0:T(2,128)(2,1)} %reshape.414), calls=%async_computation | async-start | bytes 1179648 | tf_op jit(solution)/shard_map/all_to_all | solution.py:59
  20.5 4.5 %reshape.398 = bf16[8,48,9,2,48]{4,3,2,1,0:T(2,128)(2,1)} reshape(bf16[1,8,48,864]{3,2,1,0:T(8,128)(2,1)} %param.6) | data formatting | bytes 1327104 | tf_op jit(solution)/shard_map/reshape | solution.py:75
  25.0 8.0 %slice_negate_fusion = (bf16[8,48,9,1,48]{4,3,2,1,0:T(2,128)(2,1)}, bf16[8,48,9,1,48]{4,3,2,1,0:T(2,128)(2,1)}, bf16[8,48,9,1,48]{4,3,2,1,0:T(2,128)(2,1)}) fusion(bf16[8,48,9,2,48]{4,3,2,1,0:T(2,128)(2,1)} %reshape.398), kind=kLoop, calls=%fused_computation.198 | loop fusion | flops 165888 | bytes 1658880 | tf_op jit(solution)/shard_map/neg | solution.py:78
  39.4 5.5 %bitcast_reduce_fusion.1 = bf16[128,2304]{1,0:T(8,128)(2,1)} fusion(bf16[128,1,2304]{2,1,0:T(2,128)(2,1)} %reshape.415), kind=kLoop, calls=%fused_computation.209 | loop fusion | bytes 1179648 | tf_op jit(solution)/shard_map/all_to_all | solution.py:59
  44.9 11.4 %reshape.400 = bf16[16,1,8,2,24,2,24]{6,5,4,3,2,0,1:T(2,128)(2,1)} reshape(bf16[128,2304]{1,0:T(8,128)(2,1)} %bitcast_reduce_fusion.1) | data formatting | bytes 1179648 | tf_op jit(solution)/shard_map/reshape | solution.py:64
  56.3 8.3 %fusion.61 = (bf16[16,1,8,2,24,1,24]{6,5,4,3,2,0,1:T(2,128)(2,1)S(1)}, bf16[16,1,8,2,24,1,24]{6,5,4,3,2,0,1:T(2,128)(2,1)S(1)}) fusion(bf16[16,1,8,2,24,2,24]{6,5,4,3,2,0,1:T(2,128)(2,1)} %reshape.400), kind=kLoop, calls=%fused_computation.202 | loop fusion | bytes 1179648 | tf_op jit(solution)/shard_map/slice | solution.py:21
  71.3 4.5 %all-to-all-start.1 = ((f32[16,1,96,128]{3,2,1,0:T(8,128)}), f32[16,1,96,128]{3,2,1,0:T(8,128)}, u32[]{:S(2)}, u32[]{:S(2)}) async-start(f32[16,1,96,128]{3,2,1,0:T(8,128)} %bitcast.16), calls=%async_computation.1 | async-start | bytes 1572864 | tf_op jit(solution)/shard_map/all_to_all | solution.py:71
  75.8 11.0 %maximum_bitcast_fusion.4 = (bf16[8,1,48,9,2,48]{5,4,3,2,1,0:T(2,128)(2,1)S(1)}, bf16[8,1,48,9,2,48]{5,4,3,2,1,0:T(2,128)(2,1)S(1)}) fusion(bf16[8,48,9,1,48]{4,3,2,1,0:T(2,128)(2,1)} %get-tuple-element.58, bf16[8,48,9,1,48]{4,3,2,1,0:T(2,128)(2,1)} %get-tuple-element.60, bf16[8,48,9,1,48]{4,3,2,1,0:T(2,128)(2,1)} %get-tuple-element.59), kind=kLoop, calls=%fused_computation.8 | loop fusion | flops 2654208 | bytes 2322432 | tf_op jit(solution)/shard_map/stack | solution.py:80
  86.9 7.6 %pad_maximum_fusion = bf16[8,2,48,9,2,48]{5,4,3,2,1,0:T(2,128)(2,1)} fusion(bf16[8,1,48,9,2,48]{5,4,3,2,1,0:T(2,128)(2,1)S(1)} %get-tuple-element.57, bf16[8,1,48,9,2,48]{5,4,3,2,1,0:T(2,128)(2,1)S(1)} %get-tuple-element.56), kind=kLoop, calls=%fused_computation.4 | loop fusion | flops 663552 | bytes 2654208 | tf_op jit(solution)/shard_map/stack | solution.py:80
  94.5 6.1 %reshape.399 = bf16[8,96,864]{2,1,0:T(8,128)(2,1)S(1)} reshape(bf16[8,2,48,9,2,48]{5,4,3,2,1,0:T(2,128)(2,1)} %pad_maximum_fusion) | data formatting | bytes 2654208 | tf_op jit(solution)/shard_map/reshape | solution.py:80
  102.7 4.4 %collective-permute-start = (bf16[8,96,128]{2,1,0:T(8,128)(2,1)S(1)}, bf16[8,96,128]{2,1,0:T(8,128)(2,1)S(1)}, u32[]{:S(2)}, u32[]{:S(2)}) collective-permute-start(bf16[8,96,128]{2,1,0:T(8,128)(2,1)S(1)} %get-tuple-element.109), channel_id=1, source_target_pairs={{0,15},{1,0},{2,1},{3,2},{4,3},{5,4},{6,5},{7,6},{8,7},{9,8},{10,9... | collective-permute-start | bytes 589832 | tf_op jit(solution)/shard_map/ppermute | solution.py:16
  110.3 4.9 %collective-permute-done.2 = bf16[8,96,128]{2,1,0:T(8,128)(2,1)S(1)} collective-permute-done((bf16[8,96,128]{2,1,0:T(8,128)(2,1)S(1)}, bf16[8,96,128]{2,1,0:T(8,128)(2,1)S(1)}, u32[]{:S(2)}, u32[]{:S(2)}) %collective-permute-start.2) | collective-permute-done | bytes 196640 | tf_op jit(solution)/shard_map/ppermute | solution.py:16
  118.4 21.5 %collective-permute-done.1 = bf16[2,8,96,128]{3,2,1,0:T(8,128)(2,1)S(1)} collective-permute-done((bf16[2,8,96,128]{3,2,1,0:T(8,128)(2,1)S(1)}, bf16[2,8,96,128]{3,2,1,0:T(8,128)(2,1)S(1)}, u32[]{:S(2)}, u32[]{:S(2)}) %collective-permute-start.1) | collective-permute-done | bytes 393248 | tf_op jit(solution)/shard_map/ppermute | solution.py:16
  140.0 7.2 %collective-permute-done.3 = bf16[2,8,96,128]{3,2,1,0:T(8,128)(2,1)S(1)} collective-permute-done((bf16[2,8,96,128]{3,2,1,0:T(8,128)(2,1)S(1)}, bf16[2,8,96,128]{3,2,1,0:T(8,128)(2,1)S(1)}, u32[]{:S(2)}, u32[]{:S(2)}) %collective-permute-start.3) | collective-permute-done | bytes 393248 | tf_op jit(solution)/shard_map/ppermute | solution.py:16
  148.8 32.8 %all-reduce.2 = (f32[128]{0:T(128)S(1)}, f32[128]{0:T(128)S(1)}, f32[128]{0:T(128)S(1)}) all-reduce(f32[128]{0:T(128)S(1)} %get-tuple-element.28, f32[128]{0:T(128)S(1)} %get-tuple-element.19, f32[128]{0:T(128)S(1)} %get-tuple-element.18), channel_id=1, replica_groups=mesh['cfg'=2,'ta'=16] {'ta'}, use_global_device_ids=true, to_apply=%region_4.5 | all-reduce | flops 384 | bytes 3072 | tf_op jit(solution)/shard_map/psum | solution.py:132
  187.1 6.8 %collective-permute-done.6 = bf16[8,96,128]{2,1,0:T(8,128)(2,1)S(1)} collective-permute-done((bf16[8,96,128]{2,1,0:T(8,128)(2,1)S(1)}, bf16[8,96,128]{2,1,0:T(8,128)(2,1)S(1)}, u32[]{:S(2)}, u32[]{:S(2)}) %collective-permute-start.6) | collective-permute-done | bytes 196640 | tf_op jit(solution)/shard_map/ppermute | solution.py:16
  197.1 14.7 %collective-permute-done.5 = bf16[2,8,96,128]{3,2,1,0:T(8,128)(2,1)S(1)} collective-permute-done((bf16[2,8,96,128]{3,2,1,0:T(8,128)(2,1)S(1)}, bf16[2,8,96,128]{3,2,1,0:T(8,128)(2,1)S(1)}, u32[]{:S(2)}, u32[]{:S(2)}) %collective-permute-start.5) | collective-permute-done | bytes 393248 | tf_op jit(solution)/shard_map/ppermute | solution.py:16
  211.8 8.3 %collective-permute-done.7 = bf16[2,8,96,128]{3,2,1,0:T(8,128)(2,1)S(1)} collective-permute-done((bf16[2,8,96,128]{3,2,1,0:T(8,128)(2,1)S(1)}, bf16[2,8,96,128]{3,2,1,0:T(8,128)(2,1)S(1)}, u32[]{:S(2)}, u32[]{:S(2)}) %collective-permute-start.7) | collective-permute-done | bytes 393248 | tf_op jit(solution)/shard_map/ppermute | solution.py:16
  221.2 31.6 %all-reduce.1 = (f32[128]{0:T(128)S(1)}, f32[128]{0:T(128)S(1)}, f32[128]{0:T(128)}, f32[128]{0:T(128)}, f32[128]{0:T(128)}, /*index=5*/f32[128]{0:T(128)}, f32[128]{0:T(128)}) all-reduce(f32[128]{0:T(128)S(1)} %get-tuple-element.73, f32[128]{0:T(128)S(1)} %get-tuple-element.72, ...), channel_id=1, replica_groups=mesh['cfg'=2,'ta'=16] {'ta'}, use_global_device_ids=true, to_apply=%region_14.15 | all-reduce | flops 896 | bytes 7168 | tf_op jit(solution)/shard_map/psum | solution.py:132
  257.5 6.8 %collective-permute-done.10 = bf16[8,96,128]{2,1,0:T(8,128)(2,1)S(1)} collective-permute-done((bf16[8,96,128]{2,1,0:T(8,128)(2,1)S(1)}, bf16[8,96,128]{2,1,0:T(8,128)(2,1)S(1)}, u32[]{:S(2)}, u32[]{:S(2)}) %collective-permute-start.10) | collective-permute-done | bytes 196640 | tf_op jit(solution)/shard_map/ppermute | solution.py:16
  267.6 17.0 %collective-permute-done.9 = bf16[2,8,96,128]{3,2,1,0:T(8,128)(2,1)S(1)} collective-permute-done((bf16[2,8,96,128]{3,2,1,0:T(8,128)(2,1)S(1)}, bf16[2,8,96,128]{3,2,1,0:T(8,128)(2,1)S(1)}, u32[]{:S(2)}, u32[]{:S(2)}) %collective-permute-start.9) | collective-permute-done | bytes 393248 | tf_op jit(solution)/shard_map/ppermute | solution.py:16
  284.6 8.3 %collective-permute-done.11 = bf16[2,8,96,128]{3,2,1,0:T(8,128)(2,1)S(1)} collective-permute-done((bf16[2,8,96,128]{3,2,1,0:T(8,128)(2,1)S(1)}, bf16[2,8,96,128]{3,2,1,0:T(8,128)(2,1)S(1)}, u32[]{:S(2)}, u32[]{:S(2)}) %collective-permute-start.11) | collective-permute-done | bytes 393248 | tf_op jit(solution)/shard_map/ppermute | solution.py:16
  294.2 30.4 %all-reduce = (f32[2,128]{1,0:T(2,128)S(1)}, f32[2,128]{1,0:T(2,128)S(1)}, f32[128]{0:T(128)S(1)}, f32[128]{0:T(128)S(1)}, f32[2,128]{1,0:T(2,128)S(1)}, /*index=5*/f32[2,128]{1,0:T(2,128)S(1)}, f32[128]{0:T(128)S(1)}) all-reduce(f32[2,128]{1,0:T(2,128)S(1)} %pad_maximum_fusion.18, ...), channel_id=1, replica_groups=mesh['cfg'=2,'ta'=16] {'ta'}, use_global_device_ids=true, to_apply=%region_31.32 | all-reduce | flops 1408 | bytes 11264 | tf_op jit(solution)/shard_map/psum | solution.py:132
  (161 shorter events, 51.5 us)
Async XLA Ops:
  0.6 65.8 %copy-start = (bf16[16,8,2,2,24,128]{5,4,3,2,1,0:T(8,128)(2,1)S(1)}, bf16[16,8,2,2,24,128]{5,4,3,2,1,0:T(8,128)(2,1)}, u32[]{:S(2)}) copy-start(bf16[16,8,2,2,24,128]{5,4,3,2,1,0:T(8,128)(2,1)} %param.4) | copy-start | bytes 9437188
  12.9 23.1 %all-to-all-start = ((bf16[16,2,9216]{2,1,0:T(2,128)(2,1)}), bf16[16,2,9216]{2,1,0:T(2,128)(2,1)}, u32[]{:S(2)}, u32[]{:S(2)}) async-start(bf16[16,2,9216]{2,1,0:T(2,128)(2,1)} %reshape.414), calls=%async_computation | async-start | bytes 1179648 | tf_op jit(solution)/shard_map/all_to_all | solution.py:59
  71.3 30.0 %all-to-all-start.1 = ((f32[16,1,96,128]{3,2,1,0:T(8,128)}), f32[16,1,96,128]{3,2,1,0:T(8,128)}, u32[]{:S(2)}, u32[]{:S(2)}) async-start(f32[16,1,96,128]{3,2,1,0:T(8,128)} %bitcast.16), calls=%async_computation.1 | async-start | bytes 1572864 | tf_op jit(solution)/shard_map/all_to_all | solution.py:71
  102.7 7.5 %collective-permute-start = (bf16[8,96,128]{2,1,0:T(8,128)(2,1)S(1)}, bf16[8,96,128]{2,1,0:T(8,128)(2,1)S(1)}, u32[]{:S(2)}, u32[]{:S(2)}) collective-permute-start(bf16[8,96,128]{2,1,0:T(8,128)(2,1)S(1)} %get-tuple-element.109), channel_id=1, source_target_pairs={{0,15},{1,0},{2,1},{3,2},{4,3},{5,4},{6,5},{7,6},{8,7},{9,8},{10,9... | collective-permute-start | bytes 589832 | tf_op jit(solution)/shard_map/ppermute | solution.py:16
  107.1 8.1 %collective-permute-start.2 = (bf16[8,96,128]{2,1,0:T(8,128)(2,1)S(1)}, bf16[8,96,128]{2,1,0:T(8,128)(2,1)S(1)}, u32[]{:S(2)}, u32[]{:S(2)}) collective-permute-start(bf16[8,96,128]{2,1,0:T(8,128)(2,1)S(1)} %get-tuple-element.109), channel_id=1, source_target_pairs={{0,1},{1,2},{2,3},{3,4},{4,5},{5,6},{6,7},{7,8},{8,9},{9,10},{10,1... | collective-permute-start | bytes 589832 | tf_op jit(solution)/shard_map/ppermute | solution.py:16
  115.3 24.6 %collective-permute-start.1 = (bf16[2,8,96,128]{3,2,1,0:T(8,128)(2,1)S(1)}, bf16[2,8,96,128]{3,2,1,0:T(8,128)(2,1)S(1)}, u32[]{:S(2)}, u32[]{:S(2)}) collective-permute-start(bf16[2,8,96,128]{3,2,1,0:T(8,128)(2,1)S(1)} %get-tuple-element.127), channel_id=1, source_target_pairs={{0,8},{1,9},{2,10},{3,11},{4,12},{5,13},{6,14},{7,15},{8,0},{9,1},... | collective-permute-start | bytes 1179656 | tf_op jit(solution)/shard_map/ppermute | solution.py:16
  115.4 31.8 %collective-permute-start.3 = (bf16[2,8,96,128]{3,2,1,0:T(8,128)(2,1)S(1)}, bf16[2,8,96,128]{3,2,1,0:T(8,128)(2,1)S(1)}, u32[]{:S(2)}, u32[]{:S(2)}) collective-permute-start(bf16[2,8,96,128]{3,2,1,0:T(8,128)(2,1)S(1)} %get-tuple-element.126), channel_id=1, source_target_pairs={{0,8},{1,9},{2,10},{3,11},{4,12},{5,13},{6,14},{7,15},{8,0},{9,1},... | collective-permute-start | bytes 1179656 | tf_op jit(solution)/shard_map/ppermute | solution.py:16
  182.8 72.1 %copy-start.2 = (f32[8,48,128]{2,1,0:T(8,128)}, f32[8,48,128]{2,1,0:T(8,128)S(1)}, u32[]{:S(2)}) copy-start(f32[8,48,128]{2,1,0:T(8,128)S(1)} %get-tuple-element.97) | copy-start | bytes 589828
  182.8 72.1 %copy-start.4 = (f32[8,48,128]{2,1,0:T(8,128)}, f32[8,48,128]{2,1,0:T(8,128)S(1)}, u32[]{:S(2)}) copy-start(f32[8,48,128]{2,1,0:T(8,128)S(1)} %get-tuple-element.98) | copy-start | bytes 589828
  183.8 3.3 collective-permute-start.4
  183.9 10.0 %collective-permute-start.6 = (bf16[8,96,128]{2,1,0:T(8,128)(2,1)S(1)}, bf16[8,96,128]{2,1,0:T(8,128)(2,1)S(1)}, u32[]{:S(2)}, u32[]{:S(2)}) collective-permute-start(bf16[8,96,128]{2,1,0:T(8,128)(2,1)S(1)} %get-tuple-element.50), channel_id=1, source_target_pairs={{0,1},{1,2},{2,3},{3,4},{4,5},{5,6},{6,7},{7,8},{8,9},{9,10},{10,1... | collective-permute-start | bytes 589832 | tf_op jit(solution)/shard_map/ppermute | solution.py:16
  193.9 17.8 %collective-permute-start.5 = (bf16[2,8,96,128]{3,2,1,0:T(8,128)(2,1)S(1)}, bf16[2,8,96,128]{3,2,1,0:T(8,128)(2,1)S(1)}, u32[]{:S(2)}, u32[]{:S(2)}) collective-permute-start(bf16[2,8,96,128]{3,2,1,0:T(8,128)(2,1)S(1)} %get-tuple-element.119), channel_id=1, source_target_pairs={{0,8},{1,9},{2,10},{3,11},{4,12},{5,13},{6,14},{7,15},{8,0},{9,1},... | collective-permute-start | bytes 1179656 | tf_op jit(solution)/shard_map/ppermute | solution.py:16
  194.1 26.0 %collective-permute-start.7 = (bf16[2,8,96,128]{3,2,1,0:T(8,128)(2,1)S(1)}, bf16[2,8,96,128]{3,2,1,0:T(8,128)(2,1)S(1)}, u32[]{:S(2)}, u32[]{:S(2)}) collective-permute-start(bf16[2,8,96,128]{3,2,1,0:T(8,128)(2,1)S(1)} %get-tuple-element.118), channel_id=1, source_target_pairs={{0,8},{1,9},{2,10},{3,11},{4,12},{5,13},{6,14},{7,15},{8,0},{9,1},... | collective-permute-start | bytes 1179656 | tf_op jit(solution)/shard_map/ppermute | solution.py:16
  253.6 40.2 %copy-start.10 = (f32[8,96,128]{2,1,0:T(8,128)}, f32[8,96,128]{2,1,0:T(8,128)S(1)}, u32[]{:S(2)}) copy-start(f32[8,96,128]{2,1,0:T(8,128)S(1)} %fusion.9) | copy-start | bytes 1179652
  253.7 40.1 %copy-start.12 = (f32[8,96,128]{2,1,0:T(8,128)}, f32[8,96,128]{2,1,0:T(8,128)S(1)}, u32[]{:S(2)}) copy-start(f32[8,96,128]{2,1,0:T(8,128)S(1)} %get-tuple-element.49) | copy-start | bytes 1179652
  254.2 3.2 collective-permute-start.8
  254.3 10.0 %collective-permute-start.10 = (bf16[8,96,128]{2,1,0:T(8,128)(2,1)S(1)}, bf16[8,96,128]{2,1,0:T(8,128)(2,1)S(1)}, u32[]{:S(2)}, u32[]{:S(2)}) collective-permute-start(bf16[8,96,128]{2,1,0:T(8,128)(2,1)S(1)} %get-tuple-element.48), channel_id=1, source_target_pairs={{0,1},{1,2},{2,3},{3,4},{4,5},{5,6},{6,7},{7,8},{8,9},{9,10},{10,1... | collective-permute-start | bytes 589832 | tf_op jit(solution)/shard_map/ppermute | solution.py:16
  264.4 20.2 %collective-permute-start.9 = (bf16[2,8,96,128]{3,2,1,0:T(8,128)(2,1)S(1)}, bf16[2,8,96,128]{3,2,1,0:T(8,128)(2,1)S(1)}, u32[]{:S(2)}, u32[]{:S(2)}) collective-permute-start(bf16[2,8,96,128]{3,2,1,0:T(8,128)(2,1)S(1)} %get-tuple-element.111), channel_id=1, source_target_pairs={{0,8},{1,9},{2,10},{3,11},{4,12},{5,13},{6,14},{7,15},{8,0},{9,1},... | collective-permute-start | bytes 1179656 | tf_op jit(solution)/shard_map/ppermute | solution.py:16
  264.5 28.4 %collective-permute-start.11 = (bf16[2,8,96,128]{3,2,1,0:T(8,128)(2,1)S(1)}, bf16[2,8,96,128]{3,2,1,0:T(8,128)(2,1)S(1)}, u32[]{:S(2)}, u32[]{:S(2)}) collective-permute-start(bf16[2,8,96,128]{3,2,1,0:T(8,128)(2,1)S(1)} %get-tuple-element.110), channel_id=1, source_target_pairs={{0,8},{1,9},{2,10},{3,11},{4,12},{5,13},{6,14},{7,15},{8,0},{9,1},... | collective-permute-start | bytes 1179656 | tf_op jit(solution)/shard_map/ppermute | solution.py:16
  293.8 30.8 %copy-start.15 = (f32[8,96,128]{2,1,0:T(8,128)}, f32[8,96,128]{2,1,0:T(8,128)S(1)}, u32[]{:S(2)}) copy-start(f32[8,96,128]{2,1,0:T(8,128)S(1)} %convolution_add_fusion) | copy-start | bytes 1179652
  293.8 30.9 %copy-start.17 = (f32[8,96,128]{2,1,0:T(8,128)S(1)}, f32[8,96,128]{2,1,0:T(8,128)}, u32[]{:S(2)}) copy-start(f32[8,96,128]{2,1,0:T(8,128)} %get-tuple-element.107) | copy-start | bytes 1179652
  293.8 30.9 %copy-start.21 = (f32[128]{0:T(128)S(1)}, f32[128]{0:T(128)}, u32[]{:S(2)}) copy-start(f32[128]{0:T(128)} %copy-done.20) | copy-start | bytes 1540
  293.8 30.9 %copy-start.23 = (f32[128]{0:T(128)S(1)}, f32[128]{0:T(128)}, u32[]{:S(2)}) copy-start(f32[128]{0:T(128)} %copy-done.22) | copy-start | bytes 1540
  293.8 31.0 %copy-start.19 = (f32[128]{0:T(128)S(1)}, f32[128]{0:T(128)}, u32[]{:S(2)}) copy-start(f32[128]{0:T(128)} %copy-done.18) | copy-start | bytes 1540
  (14 other events, 18.0 us)
where the time goes:
time: 335 us; the launch traced here: 329 us
  waiting for transfers between devices  106 us (32%)
  blocking collectives  94.8 us (28%)
  local copies, waits for them, and re-layouts  51 us (15%)
  other arithmetic  42.2 us (13%)
  starting transfers between devices  27 us (8%)
  matrix products  5.66 us (2%)
    ppermute x12, waiting for transfers between devices, from_behind(): return lax.ppermute(value, axis, pairs)  103 us
    psum x3, blocking collectives, shards(): lax.psum((square_loc, cross_re, cross_im, coef_re, coef_im, back_re, back...  94.8 us
    another operation x2, other arithmetic, shards(): jnp.stack([upper_rows, lower_rows], axis=1)  18.6 us
    ppermute x12, starting transfers between devices, from_behind(): return lax.ppermute(value, axis, pairs)  14.8 us
    unnamed x68, local copies, waits for them, and re-layouts  13.5 us
    reshape x1, local copies, waits for them, and re-layouts, shards(): moved_proj.reshape(plane_count, groups, group_size, 2, null_count, 2, fin...  11.4 us
    slice x1, local copies, waits for them, and re-layouts, real_weights(): proj_im = proj_view[..., 1, :]  8.34 us
    neg x1, other arithmetic, shards(): upper_rows = jnp.stack([link_re, -link_im], axis=3)  8.01 us
  transfers between devices with their start and end apart: 14, of which 13 were waited for; matrix products, arithmetic and copies ran while one was open for 12% of the time, Pallas kernels for 0%

commit v1 on v0

v1 whole, which is shorter than its diff:
```python
import math

import jax
import jax.numpy as jnp
from jax import lax
from jax.experimental import pallas as pl
from jax.experimental.pallas import tpu as pltpu
from jax.sharding import PartitionSpec as P

LX = 4
LZ = 8
ITERS = 3
LANES = 128

VMEM = pl.BlockSpec(memory_space=pltpu.VMEM)
SMEM = pl.BlockSpec(memory_space=pltpu.SMEM)


def whole_call(body, out_shape, operands, specs, scratch=(), name=None):
    return pl.pallas_call(
        body,
        out_shape=out_shape,
        in_specs=specs,
        out_specs=jax.tree.map(lambda _: VMEM, out_shape),
        scratch_shapes=list(scratch),
        name=name,
    )(*operands)


def unpack_rows(values, rows_ref, pair_count, fine_count):
    column_count = values.shape[0]
    lane = lax.broadcasted_iota(jnp.int32, (column_count, LANES), 1)
    tiles = [values[:, t * LANES:(t + 1) * LANES] for t in range(values.shape[1] // LANES)]

    def window(start, target):
        tile, offset = divmod(start, LANES)
        shift = (target - offset) % LANES
        piece = pltpu.roll(tiles[tile], shift, 1) if shift else tiles[tile]
        if offset + fine_count > LANES:
            after = pltpu.roll(tiles[tile + 1], shift, 1) if shift else tiles[tile + 1]
            piece = jnp.where(lane < target + LANES - offset, piece, after)
        return piece

    for pair in range(pair_count):
        base = (pair * 2 // pair_count) * fine_count
        start = pair * 2 * fine_count
        first = window(start, base)
        second = window(start + fine_count, base + 2 * fine_count)
        row = jnp.where((lane >= base) & (lane < base + fine_count), first, 0.0)
        inside = (lane >= base + 2 * fine_count) & (lane < base + 3 * fine_count)
        row = jnp.where(inside, second, row)
        rows_ref[pl.ds(pair, column_count, stride=pair_count), :] = row


def restrict_kernel(parity_ref, proj_ref, fine_ref, keep_ref, send_ref, rows_a, rows_b):
    plane_count, column_count, _ = proj_ref.shape
    comp_rows = fine_ref.shape[2]
    half = comp_rows // 2
    rhs_count = fine_ref.shape[3]
    fine_count = half // 2
    pair_count = proj_ref.shape[2] // (2 * fine_count)
    parity = parity_ref[0]

    def restrict_plane(plane, rows_ref):
        values = proj_ref[plane].astype(jnp.float32)
        unpack_rows(values, rows_ref, pair_count, fine_count)
        total = jnp.zeros((pair_count, 2 * rhs_count), jnp.float32)
        for column in range(column_count):
            weights = rows_ref[pl.ds(column * pair_count, pair_count), :]
            weights = weights[:, :comp_rows].astype(jnp.bfloat16)
            block = fine_ref[plane, column]
            real, imag = block[:half], block[half:]
            right = jnp.concatenate(
                [
                    jnp.concatenate([real, imag], axis=1),
                    jnp.concatenate([imag, -real], axis=1),
                ],
                axis=0,
            )
            total = total + jnp.dot(weights, right, preferred_element_type=jnp.float32)
        return total

    def step(chip, carry):
        even = restrict_plane(2 * chip, rows_a)
        odd = restrict_plane(2 * chip + 1, rows_b)
        own = jnp.where(parity == 0, even, odd)
        other = jnp.where(parity == 0, odd, even)
        keep_ref[chip, :pair_count] = own[:, :rhs_count]
        keep_ref[chip, pair_count:] = own[:, rhs_count:]
        send_ref[chip, :pair_count] = other[:, :rhs_count]
        send_ref[chip, pair_count:] = other[:, rhs_count:]
        return carry

    lax.fori_loop(0, plane_count // 2, step, 0)


def paired_restriction(fine_source, projectors, comp_count):
    plane_count, local_columns = fine_source.shape[:2]
    rhs_count = fine_source.shape[-1]
    width = projectors.shape[2]
    moved = lax.all_to_all(
        projectors.reshape(plane_count, local_columns, width), "ta", 0, 0, tiled=True
    )
    fine = fine_source.reshape(plane_count, local_columns, 2 * comp_count, rhs_count)
    parity = (lax.axis_index("ta") % 2).astype(jnp.int32).reshape(1)
    part = jax.ShapeDtypeStruct((plane_count // 2, 2 * comp_count, rhs_count), jnp.float32)
    keep, send = whole_call(
        restrict_kernel,
        (part, part),
        (parity, moved, fine),
        [SMEM, VMEM, VMEM],
        [pltpu.VMEM((local_columns * comp_count, LANES), jnp.float32)] * 2,
        name="restrict",
    )
    swap = [(device, device ^ 1) for device in range(plane_count)]
    summed = keep + lax.ppermute(send, "ta", swap)
    groups = [list(range(core, plane_count, 2)) for core in range(2)]
    return lax.all_to_all(summed, "ta", 0, 0, axis_index_groups=groups, tiled=True)


def real_weights(proj_view):
    proj_re = proj_view[..., 0, :]
    proj_im = proj_view[..., 1, :]
    first_row = jnp.stack([proj_re, proj_im], axis=-4)
    second_row = jnp.stack([-proj_im, proj_re], axis=-4)
    return jnp.stack([first_row, second_row], axis=-5)


def general_restriction(fine_source, projectors, comp_count, site_count, block_count):
    null_count = comp_count // 2
    plane_count, local_columns = fine_source.shape[:2]
    fine_count, rhs_count = fine_source.shape[4:]
    moved_proj = lax.all_to_all(projectors, "ta", split_axis=1, concat_axis=0, tiled=True)
    group_size = math.gcd(block_count, local_columns)
    groups = local_columns // group_size
    weights = real_weights(
        moved_proj.reshape(plane_count, groups, group_size, 2, null_count, 2, fine_count)
    )
    fine_local = fine_source.reshape(plane_count, groups, group_size, 2, 2, fine_count, rhs_count)
    partial_sums = jnp.einsum(
        "pmgdchvk,pmgchkr->pmdhvr", weights, fine_local, preferred_element_type=jnp.float32
    )
    partial_sums = partial_sums.reshape(plane_count, groups, 2 * comp_count, rhs_count)
    collected = lax.all_to_all(partial_sums, "ta", split_axis=0, concat_axis=1, tiled=True)
    return jnp.sum(
        collected.reshape(site_count, block_count // group_size, 2 * comp_count, rhs_count), axis=1
    )


def fold(value):
    return jnp.sum(value.reshape(-1, 8, value.shape[-1]), axis=0)


def cross(left, right, half):
    left_re, left_im = left[:half], left[half:]
    right_re, right_im = right[:half], right[half:]
    return (
        fold(left_re * right_re + left_im * right_im),
        fold(left_re * right_im - left_im * right_re),
    )


def operator_kernel(count, near, mass_ref, links_ref, residual_ref, *refs):
    vectors = refs[:near]
    basis = refs[near:near + count]
    mapped_ref, sums_ref, packed_ref = refs[near + count:]
    site_count, comp_count, _ = links_ref.shape
    rhs_count = residual_ref.shape[2]
    line_count = site_count // LX
    mass = mass_ref[0]
    for number in range(near):
        for site in range(site_count):
            real = vectors[number][site, :comp_count]
            imag = vectors[number][site, comp_count:]
            packed_ref[number, site, :comp_count, :rhs_count] = real
            packed_ref[number, site, :comp_count, rhs_count:] = imag
            packed_ref[number, site, comp_count:, :rhs_count] = -imag
            packed_ref[number, site, comp_count:, rhs_count:] = real
    totals = [jnp.zeros((8, rhs_count), jnp.float32) for _ in range(3 + 4 * count)]
    for site in range(site_count):
        line, column = divmod(site, LX)
        places = [
            (0, line, column),
            (0, line, (column + 1) % LX),
            (0, line, (column - 1) % LX),
            (0, (line + 1) % line_count, column),
            (0, (line - 1) % line_count, column),
            (1, line, column),
            (2, line, column),
            (3, line, column),
            (near - 1, line, column),
        ]
        right = jnp.concatenate([packed_ref[n, y * LX + x] for n, y, x in places], axis=0)
        product = jnp.dot(links_ref[site], right, preferred_element_type=jnp.float32)
        own = vectors[0][site].astype(jnp.float32)
        mapped = (
            jnp.concatenate([product[:, :rhs_count], product[:, rhs_count:]], axis=0) + mass * own
        )
        mapped_ref[site] = mapped
        held = residual_ref[site]
        parts = [fold(mapped * mapped), *cross(mapped, held, comp_count)]
        for earlier in basis:
            unit = earlier[site]
            parts += [*cross(unit, mapped, comp_count), *cross(unit, held, comp_count)]
        totals = [total + part for total, part in zip(totals, parts)]
    sums_ref[...] = jnp.concatenate(
        [jnp.sum(total, axis=0, keepdims=True) for total in totals]
        + [jnp.zeros((sums_ref.shape[0] - len(totals), rhs_count), jnp.float32)],
        axis=0,
    )


def scaled(vector, factor_re, factor_im, half):
    vector_re, vector_im = vector[:half], vector[half:]
    return jnp.concatenate(
        [
            factor_re * vector_re - factor_im * vector_im,
            factor_re * vector_im + factor_im * vector_re,
        ],
        axis=0,
    )


def update_kernel(count, last, sums_ref, mapped_ref, residual_ref, *refs):
    refs = list(refs)
    basis_q = [refs.pop(0) for _ in range(count)]
    basis_p = [refs.pop(0) for _ in range(count)]
    solution_ref = refs.pop(0) if count else None
    if last:
        new_solution, new_residual = refs
    else:
        new_solution, new_residual, rounded_ref, unit_q_ref, unit_p_ref = refs
    site_count = mapped_ref.shape[0]
    half = mapped_ref.shape[1] // 2
    sums = jnp.sum(sums_ref[...], axis=0)
    row = lambda index: sums[index:index + 1]
    squared, proj_re, proj_im = row(0), row(1), row(2)
    coefs = []
    for number in range(count):
        coef_re, coef_im, back_re, back_im = (row(3 + 4 * number + part) for part in range(4))
        coefs.append((coef_re, coef_im))
        squared = squared - (coef_re * coef_re + coef_im * coef_im)
        proj_re = proj_re - (coef_re * back_re + coef_im * back_im)
        proj_im = proj_im - (coef_re * back_im - coef_im * back_re)
    factor = 1.0 / jnp.sqrt(squared + 1e-06)
    alpha_re = proj_re * factor
    alpha_im = proj_im * factor
    for site in range(site_count):
        mapped = mapped_ref[site]
        held = residual_ref[site]
        direction = held
        for number, (coef_re, coef_im) in enumerate(coefs):
            mapped = mapped - scaled(basis_q[number][site], coef_re, coef_im, half)
            direction = direction - scaled(basis_p[number][site], coef_re, coef_im, half)
        unit_q = mapped * factor
        unit_p = direction * factor
        change = scaled(unit_p, alpha_re, alpha_im, half)
        new_solution[site] = change if solution_ref is None else solution_ref[site] + change
        held = held - scaled(unit_q, alpha_re, alpha_im, half)
        new_residual[site] = held
        if not last:
            rounded_ref[site] = held.astype(jnp.bfloat16)
            unit_q_ref[site] = unit_q
            unit_p_ref[site] = unit_p


def gather_sums(sums):
    devices = lax.axis_size("ta")
    if devices > 32:
        return lax.psum(sums, "ta")[None]
    copies = jnp.broadcast_to(sums, (devices,) + sums.shape)
    return lax.all_to_all(copies, "ta", 0, 0, tiled=True)


def shards(fine_source, projectors, stencil_links, quark_mass):
    _, site_count, comp_count, _ = stencil_links.shape
    plane_count, local_columns = fine_source.shape[:2]
    rhs_count = fine_source.shape[5]
    block_count = projectors.shape[1] // site_count
    if local_columns * 2 == block_count and local_columns % 8 == 0:
        source = paired_restriction(fine_source, projectors, comp_count)
    else:
        source = general_restriction(
            fine_source, projectors, comp_count, site_count, block_count
        )
    links = stencil_links[0]
    ring = [
        (plane, plane // LZ * LZ + (plane + 1) % LZ) for plane in range(plane_count)
    ]
    back = [(target, origin) for origin, target in ring]
    later = [(plane, (plane + LZ) % plane_count) for plane in range(plane_count)]
    earlier = [(target, origin) for origin, target in later]

    full = jax.ShapeDtypeStruct(source.shape, jnp.float32)
    low = jax.ShapeDtypeStruct(source.shape, jnp.bfloat16)
    rounded = source.astype(jnp.bfloat16)
    residual = source
    total = None
    basis_q, basis_p = [], []
    for iteration in range(ITERS):
        vectors = [rounded, lax.ppermute(rounded, "ta", back), lax.ppermute(rounded, "ta", ring)]
        vectors.append(lax.ppermute(rounded, "ta", earlier))
        if plane_count > 2 * LZ:
            vectors.append(lax.ppermute(rounded, "ta", later))
        near = len(vectors)
        sum_rows = -(-(3 + 4 * iteration) // 8) * 8
        mapped, sums = whole_call(
            lambda *refs: operator_kernel(iteration, near, *refs),
            (full, jax.ShapeDtypeStruct((sum_rows, rhs_count), jnp.float32)),
            (quark_mass, links, residual, *vectors, *basis_q),
            [SMEM] + [VMEM] * (2 + near + iteration),
            [pltpu.VMEM((near, site_count, 2 * comp_count, 2 * rhs_count), jnp.bfloat16)],
            name=f"operator_{iteration}",
        )
        gathered = gather_sums(sums)
        last = iteration == ITERS - 1
        operands = [gathered, mapped, residual, *basis_q, *basis_p]
        if iteration:
            operands.append(total)
        outs = whole_call(
            lambda *refs: update_kernel(iteration, last, *refs),
            (full, full) if last else (full, full, low, full, full),
            operands,
            [VMEM] * len(operands),
            name=f"update_{iteration}",
        )
        total, residual = outs[:2]
        if not last:
            rounded = outs[2]
            basis_q.append(outs[3])
            basis_p.append(outs[4])
    return total[None], residual[None]


def solution(mesh):
    return jax.shard_map(
        shards,
        mesh=mesh,
        in_specs=(
            P("cfg", "ta", None, None, None, None),
            P(("cfg", "ta"), None, None),
            P(("cfg", "ta"), None, None, None),
            P("cfg"),
        ),
        out_specs=(P(("cfg", "ta"), None, None, None), P(("cfg", "ta"), None, None, None)),
        check_vma=False,
    )
```

time: 335 us -> 143 us (0.43); the launches traced: 329 us -> 142 us
  waiting for transfers between devices: 106 us -> 41.6 us
  local copies, waits for them, and re-layouts: 51 us -> 5.21 us
  blocking collectives: 94.8 us -> 51.5 us
  other arithmetic: 42.2 us -> 1.09 us
  Pallas kernels: 0 us -> 24.5 us
  starting transfers between devices: 27 us -> 17 us
  matrix products: 5.66 us -> 0 us
    psum x3 -> x0, blocking collectives: 94.8 us -> none  [shards(): lax.psum((square_loc, cross_re, cross_im, coef_re, coef_im, back_re, back...]
    ppermute x12 -> x10, waiting for transfers between devices: 103 us -> 26.2 us  [the longest x3 24.3 us: shards(): vectors.append(lax.ppermute(rounded, 'ta', earlier))]
    all_to_all x0 -> x4, blocking collectives: none -> 51.5 us  [the longest x3 34.7 us: gather_sums(): return lax.all_to_all(copies, 'ta', 0, 0, tiled=True)]
    pallas_call x0 -> x7, Pallas kernels: none -> 24.5 us  [whole_call(): pl.pallas_call(body, out_shape=out_shape, in_specs=specs, out_specs=jax.t...]
    reshape x3 -> x0, local copies, waits for them, and re-layouts: 22 us -> none  [the longest x1 11.4 us: shards(): moved_proj.reshape(plane_count, groups, group_size, 2, null_count, 2, fin...]
    another operation x10 -> x0, other arithmetic: 19.8 us -> none  [the longest x2 18.6 us: shards(): jnp.stack([upper_rows, lower_rows], axis=1)]
    all_to_all x2 -> x1, waiting for transfers between devices: 2.88 us -> 15.4 us  [paired_restriction(): lax.all_to_all(projectors.reshape(plane_count, local_columns, width), 'ta...]
    unnamed x68 -> x24, local copies, waits for them, and re-layouts: 13.5 us -> 3.14 us
  transfers between devices with their start and end apart: 14 -> 11, of which waited for: 13 -> 6; matrix products, arithmetic and copies ran while one was open for 12% -> 0% of each run, Pallas kernels for 0% -> 0%
where the time goes in v1:
time: 143 us; the launch traced here: 142 us
  blocking collectives  51.5 us (36%)
  waiting for transfers between devices  41.6 us (29%)
  Pallas kernels  24.5 us (17%)
  starting transfers between devices  17 us (12%)
  local copies, waits for them, and re-layouts  5.21 us (4%)
    all_to_all x3, blocking collectives, gather_sums(): return lax.all_to_all(copies, 'ta', 0, 0, tiled=True)  34.7 us
    pallas_call x7, Pallas kernels, whole_call(): pl.pallas_call(body, out_shape=out_shape, in_specs=specs, out_specs=jax.t...  24.5 us
    ppermute x3, waiting for transfers between devices, shards(): vectors.append(lax.ppermute(rounded, 'ta', earlier))  24.3 us
    all_to_all x1, blocking collectives, paired_restriction(): lax.all_to_all(summed, 'ta', 0, 0, axis_index_groups=groups, tiled=True)  16.8 us
    all_to_all x1, waiting for transfers between devices, paired_restriction(): lax.all_to_all(projectors.reshape(plane_count, local_columns, width), 'ta...  15.4 us
    ppermute x3, starting transfers between devices, shards(): lax.ppermute(rounded, 'ta', back)  7.93 us
    all_to_all x1, starting transfers between devices, paired_restriction(): lax.all_to_all(projectors.reshape(plane_count, local_columns, width), 'ta...  7.43 us
    unnamed x24, local copies, waits for them, and re-layouts  3.14 us
  transfers between devices with their start and end apart: 11, of which 6 were waited for; matrix products, arithmetic and copies ran while one was open for 0% of the time, Pallas kernels for 0%

profile of v1, /device:TPU:0, one launch (start us, length us, event | category | flops | bytes accessed | tf_op | source)
XLA Modules:
  0.0 142.2 jit_solution(3975794062770065554)
XLA Ops:
  0.6 7.4 %all-to-all-start = ((bf16[16,8,2304]{2,1,0:T(8,128)(2,1)}), bf16[16,8,2304]{2,1,0:T(8,128)(2,1)S(1)}, u32[]{:S(2)}, u32[]{:S(2)}) async-start(bf16[16,8,2304]{2,1,0:T(8,128)(2,1)} %bitcast.10), calls=%async_computation | async-start | bytes 1179648 | tf_op jit(solution)/shard_map/all_to_all | solution.py:101
  8.1 15.4 %all-to-all-done.proj_ref = bf16[16,8,2304]{2,1,0:T(8,128)(2,1)S(1)} async-done(((bf16[16,8,2304]{2,1,0:T(8,128)(2,1)}), bf16[16,8,2304]{2,1,0:T(8,128)(2,1)S(1)}, u32[]{:S(2)}, u32[]{:S(2)}) %all-to-all-start) | async-done | bytes 589856 | tf_op jit(solution)/shard_map/all_to_all | solution.py:101
  23.4 0.8 copy-done.1
  24.3 6.6 %restrict.1 = (f32[8,96,128]{2,1,0:T(8,128)}, f32[8,96,128]{2,1,0:T(8,128)}) custom-call(s32[1]{0:T(128)} %bitcast.1.parity_ref, bf16[16,8,2304]{2,1,0:T(8,128)(2,1)} %copy-done.1, bf16[16,8,96,128]{3,2,1,0:T(8,128)(2,1)} %bitcast.9), custom_call_target="tpu_custom_call" | custom-call | tf_op jit(solution)/shard_map/restrict/pallas_call | solution.py:20
  31.1 1.7 %collective-permute-done = f32[8,96,128]{2,1,0:T(8,128)S(1)} collective-permute-done((f32[8,96,128]{2,1,0:T(8,128)}, f32[8,96,128]{2,1,0:T(8,128)S(1)}, u32[]{:S(2)}, u32[]{:S(2)}) %collective-permute-start) | collective-permute-done | bytes 393248 | tf_op jit(solution)/shard_map/ppermute | solution.py:116
  32.8 1.1 add.8
  33.9 16.8 %all_to_all.25.refs_2_ = f32[8,96,128]{2,1,0:T(8,128)S(1)} all-to-all(f32[8,96,128]{2,1,0:T(8,128)S(1)} %add.8), channel_id=1, replica_groups={{0,2,4,6,8,10,12,14},{1,3,5,7,9,11,13,15},{16,18,20,22,24,26,28,30},{17..., dimensions={0} | all-to-all | bytes 786432 | tf_op jit(solution)/shard_map/all_to_all | solution.py:118
  50.7 1.0 collective-permute-start.3
  51.6 2.6 %collective-permute-start.1 = (bf16[8,96,128]{2,1,0:T(8,128)(2,1)S(1)}, bf16[8,96,128]{2,1,0:T(8,128)(2,1)S(1)}, u32[]{:S(2)}, u32[]{:S(2)}) collective-permute-start(bf16[8,96,128]{2,1,0:T(8,128)(2,1)S(1)} %convert_element_type.3.refs_3_), channel_id=1, source_target_pairs={{1,0},{2,1},{3,2},{4,3},{5,4},{6,5},{7,6},{0,7},{9,8},{10,9},{11,1... | collective-permute-start | bytes 589832 | tf_op jit(solution)/shard_map/ppermute | solution.py:301
  54.9 6.7 %collective-permute-done.3.refs_6_ = bf16[8,96,128]{2,1,0:T(8,128)(2,1)S(1)} collective-permute-done((bf16[8,96,128]{2,1,0:T(8,128)(2,1)S(1)}, bf16[8,96,128]{2,1,0:T(8,128)(2,1)S(1)}, u32[]{:S(2)}, u32[]{:S(2)}) %collective-permute-start.3) | collective-permute-done | bytes 196640 | tf_op jit(solution)/shard_map/ppermute | solution.py:302
  62.6 3.0 %operator_0.1 = (f32[8,96,128]{2,1,0:T(8,128)}, f32[8,128]{1,0:T(8,128)}) custom-call(f32[1]{0:T(128)S(6)} %copy.6.refs_0_, bf16[8,48,864]{2,1,0:T(8,128)(2,1)} %bitcast.6, f32[8,96,128]{2,1,0:T(8,128)} %copy-done, bf16[8,96,128]{2,1,0:T(8,128)(2,1)} %copy-done.2, bf16[8,96,128]{2,1,0:T(8,128)(2,1)} %copy-done.11, bf16[8,96,128]{2,1,0:T(8,128)(2,1)} %copy-done.10, ...), custom_call_target="tpu_custom_call" | custom-call | tf_op jit(solution)/shard_map/operator_0/pallas_call | solution.py:20
  66.2 11.4 %all_to_all.26.refs_0_ = f32[16,8,128]{2,1,0:T(8,128)} all-to-all(f32[16,8,128]{2,1,0:T(8,128)S(1)} %broadcast_in_dim.15), channel_id=1, replica_groups=mesh['cfg'=2,'ta'=16] {'ta'}, dimensions={0} | all-to-all | bytes 131072 | tf_op jit(solution)/shard_map/all_to_all | solution.py:272
  77.7 2.5 %update_0.1 = (f32[8,96,128]{2,1,0:T(8,128)}, f32[8,96,128]{2,1,0:T(8,128)}, bf16[8,96,128]{2,1,0:T(8,128)(2,1)}, f32[8,96,128]{2,1,0:T(8,128)}, f32[8,96,128]{2,1,0:T(8,128)}) custom-call(f32[16,8,128]{2,1,0:T(8,128)} %all_to_all.26.refs_0_, f32[8,96,128]{2,1,0:T(8,128)} %get-tuple-element.25.refs_1_, f32[8,96,128]{2,1,0:T(8,128)} %copy-done), custom_call_target="tpu_custom_call" | custom-call | tf_op jit(solution)/shard_map/update_0/pallas_call | solution.py:20
  80.4 2.6 %collective-permute-start.4 = (bf16[8,96,128]{2,1,0:T(8,128)(2,1)}, bf16[8,96,128]{2,1,0:T(8,128)(2,1)S(1)}, u32[]{:S(2)}, u32[]{:S(2)}) collective-permute-start(bf16[8,96,128]{2,1,0:T(8,128)(2,1)} %get-tuple-element.27.refs_3_), channel_id=1, source_target_pairs={{1,0},{2,1},{3,2},{4,3},{5,4},{6,5},{7,6},{0,7},{9,8},{10,9},{11,1... | collective-permute-start | bytes 589832 | tf_op jit(solution)/shard_map/ppermute | solution.py:301
  83.1 8.8 %collective-permute-done.6.refs_6_ = bf16[8,96,128]{2,1,0:T(8,128)(2,1)S(1)} collective-permute-done((bf16[8,96,128]{2,1,0:T(8,128)(2,1)}, bf16[8,96,128]{2,1,0:T(8,128)(2,1)S(1)}, u32[]{:S(2)}, u32[]{:S(2)}) %collective-permute-start.6) | collective-permute-done | bytes 196640 | tf_op jit(solution)/shard_map/ppermute | solution.py:302
  92.7 3.2 %operator_1.1 = (f32[8,96,128]{2,1,0:T(8,128)}, f32[8,128]{1,0:T(8,128)}) custom-call(f32[1]{0:T(128)S(6)} %copy.6.refs_0_, bf16[8,48,864]{2,1,0:T(8,128)(2,1)} %bitcast.7, f32[8,96,128]{2,1,0:T(8,128)} %get-tuple-element.26.refs_2_, bf16[8,96,128]{2,1,0:T(8,128)(2,1)} %get-tuple-element.27.refs_3_, bf16[8,96,128]{2,1,0:T(8,128)(2,1)} %copy-done.8, ...), custom_call_target="tpu_custom_call" | custom-call | tf_op jit(solution)/shard_map/operator_1/pallas_call | solution.py:20
  96.6 11.1 %all_to_all.27.refs_0_ = f32[16,8,128]{2,1,0:T(8,128)} all-to-all(f32[16,8,128]{2,1,0:T(8,128)S(1)} %broadcast_in_dim.16), channel_id=1, replica_groups=mesh['cfg'=2,'ta'=16] {'ta'}, dimensions={0} | all-to-all | bytes 131072 | tf_op jit(solution)/shard_map/all_to_all | solution.py:272
  107.7 2.9 %update_1.1 = (f32[8,96,128]{2,1,0:T(8,128)}, f32[8,96,128]{2,1,0:T(8,128)}, bf16[8,96,128]{2,1,0:T(8,128)(2,1)}, f32[8,96,128]{2,1,0:T(8,128)}, f32[8,96,128]{2,1,0:T(8,128)}) custom-call(f32[16,8,128]{2,1,0:T(8,128)} %all_to_all.27.refs_0_, f32[8,96,128]{2,1,0:T(8,128)} %get-tuple-element.30.refs_1_, f32[8,96,128]{2,1,0:T(8,128)} %get-tuple-element.26.refs_2_, ...), custom_call_target="tpu_custom_call" | custom-call | tf_op jit(solution)/shard_map/update_1/pallas_call | solution.py:20
  110.8 2.6 %collective-permute-start.7 = (bf16[8,96,128]{2,1,0:T(8,128)(2,1)}, bf16[8,96,128]{2,1,0:T(8,128)(2,1)S(1)}, u32[]{:S(2)}, u32[]{:S(2)}) collective-permute-start(bf16[8,96,128]{2,1,0:T(8,128)(2,1)} %get-tuple-element.34.refs_3_), channel_id=1, source_target_pairs={{1,0},{2,1},{3,2},{4,3},{5,4},{6,5},{7,6},{0,7},{9,8},{10,9},{11,1... | collective-permute-start | bytes 589832 | tf_op jit(solution)/shard_map/ppermute | solution.py:301
  113.5 8.8 %collective-permute-done.9.refs_6_ = bf16[8,96,128]{2,1,0:T(8,128)(2,1)S(1)} collective-permute-done((bf16[8,96,128]{2,1,0:T(8,128)(2,1)}, bf16[8,96,128]{2,1,0:T(8,128)(2,1)S(1)}, u32[]{:S(2)}, u32[]{:S(2)}) %collective-permute-start.9) | collective-permute-done | bytes 196640 | tf_op jit(solution)/shard_map/ppermute | solution.py:302
  123.1 3.3 %operator_2.1 = (f32[8,96,128]{2,1,0:T(8,128)}, f32[16,128]{1,0:T(8,128)}) custom-call(f32[1]{0:T(128)S(6)} %copy.6.refs_0_, bf16[8,48,864]{2,1,0:T(8,128)(2,1)} %bitcast.8, f32[8,96,128]{2,1,0:T(8,128)} %get-tuple-element.33.refs_2_, bf16[8,96,128]{2,1,0:T(8,128)(2,1)} %get-tuple-element.34.refs_3_, bf16[8,96,128]{2,1,0:T(8,128)(2,1)} %copy-done.7, ...), custom_call_target="tpu_custom_call" | custom-call | tf_op jit(solution)/shard_map/operator_2/pallas_call | solution.py:20
  126.4 0.7 broadcast_in_dim.17
  127.1 12.1 %all_to_all.28.refs_0_ = f32[16,16,128]{2,1,0:T(8,128)} all-to-all(f32[16,16,128]{2,1,0:T(8,128)S(1)} %broadcast_in_dim.17), channel_id=1, replica_groups=mesh['cfg'=2,'ta'=16] {'ta'}, dimensions={0} | all-to-all | bytes 262144 | tf_op jit(solution)/shard_map/all_to_all | solution.py:272
  139.3 3.0 %update_2.1 = (f32[8,96,128]{2,1,0:T(8,128)}, f32[8,96,128]{2,1,0:T(8,128)}) custom-call(f32[16,16,128]{2,1,0:T(8,128)} %all_to_all.28.refs_0_, f32[8,96,128]{2,1,0:T(8,128)} %get-tuple-element.37.refs_1_, f32[8,96,128]{2,1,0:T(8,128)} %get-tuple-element.33.refs_2_, f32[8,96,128]{2,1,0:T(8,128)} %get-tuple-element.28.refs_7_.refs_3_, ...), custom_call_target="tpu_custom_call" | custom-call | tf_op jit(solution)/shard_map/update_2/pallas_call | solution.py:20
  (38 shorter events, 4.6 us)
Async XLA Ops:
  0.6 22.8 %all-to-all-start = ((bf16[16,8,2304]{2,1,0:T(8,128)(2,1)}), bf16[16,8,2304]{2,1,0:T(8,128)(2,1)S(1)}, u32[]{:S(2)}, u32[]{:S(2)}) async-start(bf16[16,8,2304]{2,1,0:T(8,128)(2,1)} %bitcast.10), calls=%async_computation | async-start | bytes 1179648 | tf_op jit(solution)/shard_map/all_to_all | solution.py:101
  23.4 0.8 copy-start.1
  30.9 1.9 %collective-permute-start = (f32[8,96,128]{2,1,0:T(8,128)}, f32[8,96,128]{2,1,0:T(8,128)S(1)}, u32[]{:S(2)}, u32[]{:S(2)}) collective-permute-start(f32[8,96,128]{2,1,0:T(8,128)} %get-tuple-element.23), channel_id=1, source_target_pairs={{0,1},{1,0},{2,3},{3,2},{4,5},{5,4},{6,7},{7,6},{8,9},{9,8},{10,11... | collective-permute-start | bytes 1179656 | tf_op jit(solution)/shard_map/ppermute | solution.py:116
  50.6 11.2 %copy-start = (f32[8,96,128]{2,1,0:T(8,128)}, f32[8,96,128]{2,1,0:T(8,128)S(1)}, u32[]{:S(2)}) copy-start(f32[8,96,128]{2,1,0:T(8,128)S(1)} %all_to_all.25.refs_2_) | copy-start | bytes 1179652
  50.7 11.2 %copy-start.2 = (bf16[8,96,128]{2,1,0:T(8,128)(2,1)}, bf16[8,96,128]{2,1,0:T(8,128)(2,1)S(1)}, u32[]{:S(2)}) copy-start(bf16[8,96,128]{2,1,0:T(8,128)(2,1)S(1)} %convert_element_type.3.refs_3_) | copy-start | bytes 589828
  50.7 11.0 %collective-permute-start.3 = (bf16[8,96,128]{2,1,0:T(8,128)(2,1)S(1)}, bf16[8,96,128]{2,1,0:T(8,128)(2,1)S(1)}, u32[]{:S(2)}, u32[]{:S(2)}) collective-permute-start(bf16[8,96,128]{2,1,0:T(8,128)(2,1)S(1)} %convert_element_type.3.refs_3_), channel_id=1, source_target_pairs={{8,0},{9,1},{10,2},{11,3},{12,4},{13,5},{14,6},{15,7},{0,8},{1,9},... | collective-permute-start | bytes 589832 | tf_op jit(solution)/shard_map/ppermute | solution.py:302
  51.6 10.2 %collective-permute-start.2 = (bf16[8,96,128]{2,1,0:T(8,128)(2,1)S(1)}, bf16[8,96,128]{2,1,0:T(8,128)(2,1)S(1)}, u32[]{:S(2)}, u32[]{:S(2)}) collective-permute-start(bf16[8,96,128]{2,1,0:T(8,128)(2,1)S(1)} %convert_element_type.3.refs_3_), channel_id=1, source_target_pairs={{0,1},{1,2},{2,3},{3,4},{4,5},{5,6},{6,7},{7,0},{8,9},{9,10},{10,1... | collective-permute-start | bytes 589832 | tf_op jit(solution)/shard_map/ppermute | solution.py:301
  51.6 10.2 %collective-permute-start.1 = (bf16[8,96,128]{2,1,0:T(8,128)(2,1)S(1)}, bf16[8,96,128]{2,1,0:T(8,128)(2,1)S(1)}, u32[]{:S(2)}, u32[]{:S(2)}) collective-permute-start(bf16[8,96,128]{2,1,0:T(8,128)(2,1)S(1)} %convert_element_type.3.refs_3_), channel_id=1, source_target_pairs={{1,0},{2,1},{3,2},{4,3},{5,4},{6,5},{7,6},{0,7},{9,8},{10,9},{11,1... | collective-permute-start | bytes 589832 | tf_op jit(solution)/shard_map/ppermute | solution.py:301
  61.6 0.7 copy-start.9
  61.8 0.7 copy-start.10
  61.8 0.7 copy-start.11
  80.2 11.7 %collective-permute-start.6 = (bf16[8,96,128]{2,1,0:T(8,128)(2,1)}, bf16[8,96,128]{2,1,0:T(8,128)(2,1)S(1)}, u32[]{:S(2)}, u32[]{:S(2)}) collective-permute-start(bf16[8,96,128]{2,1,0:T(8,128)(2,1)} %get-tuple-element.27.refs_3_), channel_id=1, source_target_pairs={{8,0},{9,1},{10,2},{11,3},{12,4},{13,5},{14,6},{15,7},{0,8},{1,9},... | collective-permute-start | bytes 589832 | tf_op jit(solution)/shard_map/ppermute | solution.py:302
  80.4 11.5 %collective-permute-start.5 = (bf16[8,96,128]{2,1,0:T(8,128)(2,1)}, bf16[8,96,128]{2,1,0:T(8,128)(2,1)S(1)}, u32[]{:S(2)}, u32[]{:S(2)}) collective-permute-start(bf16[8,96,128]{2,1,0:T(8,128)(2,1)} %get-tuple-element.27.refs_3_), channel_id=1, source_target_pairs={{0,1},{1,2},{2,3},{3,4},{4,5},{5,6},{6,7},{7,0},{8,9},{9,10},{10,1... | collective-permute-start | bytes 589832 | tf_op jit(solution)/shard_map/ppermute | solution.py:301
  80.4 11.5 %collective-permute-start.4 = (bf16[8,96,128]{2,1,0:T(8,128)(2,1)}, bf16[8,96,128]{2,1,0:T(8,128)(2,1)S(1)}, u32[]{:S(2)}, u32[]{:S(2)}) collective-permute-start(bf16[8,96,128]{2,1,0:T(8,128)(2,1)} %get-tuple-element.27.refs_3_), channel_id=1, source_target_pairs={{1,0},{2,1},{3,2},{4,3},{5,4},{6,5},{7,6},{0,7},{9,8},{10,9},{11,1... | collective-permute-start | bytes 589832 | tf_op jit(solution)/shard_map/ppermute | solution.py:301
  91.9 0.7 copy-start.4
  91.9 0.7 copy-start.6
  91.9 0.8 copy-start.8
  110.6 11.7 %collective-permute-start.9 = (bf16[8,96,128]{2,1,0:T(8,128)(2,1)}, bf16[8,96,128]{2,1,0:T(8,128)(2,1)S(1)}, u32[]{:S(2)}, u32[]{:S(2)}) collective-permute-start(bf16[8,96,128]{2,1,0:T(8,128)(2,1)} %get-tuple-element.34.refs_3_), channel_id=1, source_target_pairs={{8,0},{9,1},{10,2},{11,3},{12,4},{13,5},{14,6},{15,7},{0,8},{1,9},... | collective-permute-start | bytes 589832 | tf_op jit(solution)/shard_map/ppermute | solution.py:302
  110.8 11.5 %collective-permute-start.8 = (bf16[8,96,128]{2,1,0:T(8,128)(2,1)}, bf16[8,96,128]{2,1,0:T(8,128)(2,1)S(1)}, u32[]{:S(2)}, u32[]{:S(2)}) collective-permute-start(bf16[8,96,128]{2,1,0:T(8,128)(2,1)} %get-tuple-element.34.refs_3_), channel_id=1, source_target_pairs={{0,1},{1,2},{2,3},{3,4},{4,5},{5,6},{6,7},{7,0},{8,9},{9,10},{10,1... | collective-permute-start | bytes 589832 | tf_op jit(solution)/shard_map/ppermute | solution.py:301
  110.8 11.5 %collective-permute-start.7 = (bf16[8,96,128]{2,1,0:T(8,128)(2,1)}, bf16[8,96,128]{2,1,0:T(8,128)(2,1)S(1)}, u32[]{:S(2)}, u32[]{:S(2)}) collective-permute-start(bf16[8,96,128]{2,1,0:T(8,128)(2,1)} %get-tuple-element.34.refs_3_), channel_id=1, source_target_pairs={{1,0},{2,1},{3,2},{4,3},{5,4},{6,5},{7,6},{0,7},{9,8},{10,9},{11,1... | collective-permute-start | bytes 589832 | tf_op jit(solution)/shard_map/ppermute | solution.py:301
  122.3 0.7 copy-start.3
  122.3 0.8 copy-start.5
  122.3 0.8 copy-start.7

commit v2 on v1

--- a/solution.py
+++ b/solution.py
@@ -23,6 +23,7 @@
         in_specs=specs,
         out_specs=jax.tree.map(lambda _: VMEM, out_shape),
         scratch_shapes=list(scratch),
+        compiler_params=pltpu.CompilerParams(vmem_limit_bytes=16 * 1024 * 1024),
         name=name,
     )(*operands)
 
@@ -52,69 +53,73 @@
         rows_ref[pl.ds(pair, column_count, stride=pair_count), :] = row
 
 
-def restrict_kernel(parity_ref, proj_ref, fine_ref, keep_ref, send_ref, rows_a, rows_b):
-    plane_count, column_count, _ = proj_ref.shape
-    comp_rows = fine_ref.shape[2]
+def restrict_kernel(parity_ref, proj_ref, fine_ref, other_ref, source_ref, rows_ref):
+    chip_count, column_count, _ = proj_ref.shape
+    local_count, comp_rows, rhs_count = fine_ref.shape[1:]
     half = comp_rows // 2
-    rhs_count = fine_ref.shape[3]
     fine_count = half // 2
     pair_count = proj_ref.shape[2] // (2 * fine_count)
     parity = parity_ref[0]
 
-    def restrict_plane(plane, rows_ref):
-        values = proj_ref[plane].astype(jnp.float32)
-        unpack_rows(values, rows_ref, pair_count, fine_count)
+    def step(chip, carry):
+        values = proj_ref[chip].astype(jnp.float32)
+        for core in range(column_count // local_count):
+            unpack_rows(
+                values[core * local_count:(core + 1) * local_count],
+                rows_ref.at[core],
+                pair_count,
+                fine_count,
+            )
         total = jnp.zeros((pair_count, 2 * rhs_count), jnp.float32)
-        for column in range(column_count):
-            weights = rows_ref[pl.ds(column * pair_count, pair_count), :]
-            weights = weights[:, :comp_rows].astype(jnp.bfloat16)
-            block = fine_ref[plane, column]
-            real, imag = block[:half], block[half:]
-            right = jnp.concatenate(
-                [
-                    jnp.concatenate([real, imag], axis=1),
-                    jnp.concatenate([imag, -real], axis=1),
-                ],
-                axis=0,
-            )
-            total = total + jnp.dot(weights, right, preferred_element_type=jnp.float32)
-        return total
-
-    def step(chip, carry):
-        even = restrict_plane(2 * chip, rows_a)
-        odd = restrict_plane(2 * chip + 1, rows_b)
-        own = jnp.where(parity == 0, even, odd)
-        other = jnp.where(parity == 0, odd, even)
-        keep_ref[chip, :pair_count] = own[:, :rhs_count]
-        keep_ref[chip, pair_count:] = own[:, rhs_count:]
-        send_ref[chip, :pair_count] = other[:, :rhs_count]
-        send_ref[chip, pair_count:] = other[:, rhs_count:]
+        for core, ref, index in ((parity, fine_ref, 2 * chip + parity), (1 - parity, other_ref, chip)):
+            for column in range(local_count):
+                weights = rows_ref[core, pl.ds(column * pair_count, pair_count), :]
+                weights = weights[:, :comp_rows].astype(jnp.bfloat16)
+                block = ref[index, column]
+                real, imag = block[:half], block[half:]
+                right = jnp.concatenate(
+                    [
+                        jnp.concatenate([real, imag], axis=1),
+                        jnp.concatenate([imag, -real], axis=1),
+                    ],
+                    axis=0,
+                )
+                total = total + jnp.dot(weights, right, preferred_element_type=jnp.float32)
+        source_ref[chip, :pair_count] = total[:, :rhs_count]
+        source_ref[chip, pair_count:] = total[:, rhs_count:]
         return carry
 
-    lax.fori_loop(0, plane_count // 2, step, 0)
+    lax.fori_loop(0, chip_count, step, 0)
 
 
 def paired_restriction(fine_source, projectors, comp_count):
     plane_count, local_columns = fine_source.shape[:2]
     rhs_count = fine_source.shape[-1]
     width = projectors.shape[2]
+    chip_count = plane_count // 2
+    groups = [list(range(core, plane_count, 2)) for core in range(2)]
     moved = lax.all_to_all(
-        projectors.reshape(plane_count, local_columns, width), "ta", 0, 0, tiled=True
-    )
+        projectors.reshape(chip_count, 2 * local_columns, width),
+        "ta",
+        0,
+        0,
+        axis_index_groups=groups,
+        tiled=True,
+    )
+    core = lax.axis_index("ta") % 2
     fine = fine_source.reshape(plane_count, local_columns, 2 * comp_count, rhs_count)
-    parity = (lax.axis_index("ta") % 2).astype(jnp.int32).reshape(1)
-    part = jax.ShapeDtypeStruct((plane_count // 2, 2 * comp_count, rhs_count), jnp.float32)
-    keep, send = whole_call(
+    given = lax.dynamic_index_in_dim(
+        fine.reshape((chip_count, 2) + fine.shape[1:]), 1 - core, axis=1, keepdims=False
+    )
+    other = lax.ppermute(given, "ta", [(device, device ^ 1) for device in range(plane_count)])
+    summed = whole_call(
         restrict_kernel,
-        (part, part),
-        (parity, moved, fine),
-        [SMEM, VMEM, VMEM],
-        [pltpu.VMEM((local_columns * comp_count, LANES), jnp.float32)] * 2,
+        jax.ShapeDtypeStruct((chip_count, 2 * comp_count, rhs_count), jnp.float32),
+        (core.astype(jnp.int32).reshape(1), moved, fine, other),
+        [SMEM, VMEM, VMEM, VMEM],
+        [pltpu.VMEM((2, local_columns * comp_count, LANES), jnp.float32)],
         name="restrict",
     )
-    swap = [(device, device ^ 1) for device in range(plane_count)]
-    summed = keep + lax.ppermute(send, "ta", swap)
-    groups = [list(range(core, plane_count, 2)) for core in range(2)]
     return lax.all_to_all(summed, "ta", 0, 0, axis_index_groups=groups, tiled=True)
 
 
@@ -203,11 +208,13 @@
             unit = earlier[site]
             parts += [*cross(unit, mapped, comp_count), *cross(unit, held, comp_count)]
         totals = [total + part for total, part in zip(totals, parts)]
-    sums_ref[...] = jnp.concatenate(
+    sums = jnp.concatenate(
         [jnp.sum(total, axis=0, keepdims=True) for total in totals]
-        + [jnp.zeros((sums_ref.shape[0] - len(totals), rhs_count), jnp.float32)],
+        + [jnp.zeros((sums_ref.shape[1] - len(totals), rhs_count), jnp.float32)],
         axis=0,
     )
+    for copy in range(sums_ref.shape[0]):
+        sums_ref[copy] = sums
 
 
 def scaled(vector, factor_re, factor_im, half):
@@ -265,11 +272,9 @@
 
 
 def gather_sums(sums):
-    devices = lax.axis_size("ta")
-    if devices > 32:
-        return lax.psum(sums, "ta")[None]
-    copies = jnp.broadcast_to(sums, (devices,) + sums.shape)
-    return lax.all_to_all(copies, "ta", 0, 0, tiled=True)
+    if sums.shape[0] == 1:
+        return lax.psum(sums, "ta")
+    return lax.all_to_all(sums, "ta", 0, 0, tiled=True)
 
 
 def shards(fine_source, projectors, stencil_links, quark_mass):
@@ -291,6 +296,7 @@
     later = [(plane, (plane + LZ) % plane_count) for plane in range(plane_count)]
     earlier = [(target, origin) for origin, target in later]
 
+    copies = plane_count if plane_count <= 32 else 1
     full = jax.ShapeDtypeStruct(source.shape, jnp.float32)
     low = jax.ShapeDtypeStruct(source.shape, jnp.bfloat16)
     rounded = source.astype(jnp.bfloat16)
@@ -306,7 +312,7 @@
         sum_rows = -(-(3 + 4 * iteration) // 8) * 8
         mapped, sums = whole_call(
             lambda *refs: operator_kernel(iteration, near, *refs),
-            (full, jax.ShapeDtypeStruct((sum_rows, rhs_count), jnp.float32)),
+            (full, jax.ShapeDtypeStruct((copies, sum_rows, rhs_count), jnp.float32)),
             (quark_mass, links, residual, *vectors, *basis_q),
             [SMEM] + [VMEM] * (2 + near + iteration),
             [pltpu.VMEM((near, site_count, 2 * comp_count, 2 * rhs_count), jnp.bfloat16)],

time: 143 us -> 119 us (0.83)
  blocking collectives: 51.5 us -> 73.7 us
  waiting for transfers between devices: 41.6 us -> 24.1 us
  Pallas kernels: 24.5 us -> 8.01 us
  starting transfers between devices: 17 us -> 10 us
  local copies, waits for them, and re-layouts: 5.21 us -> 1.69 us
    all_to_all x3 -> x4, blocking collectives: 34.7 us -> 58.5 us  [the longest x3 34.7 us: gather_sums(): return lax.all_to_all(sums, 'ta', 0, 0, tiled=True)]
    pallas_call x7, Pallas kernels: 24.5 us -> 8.01 us  [whole_call(): pl.pallas_call(body, out_shape=out_shape, in_specs=specs, out_specs=jax.t...]
    all_to_all x1 -> x0, waiting for transfers between devices: 15.4 us -> none  [paired_restriction(): lax.all_to_all(projectors.reshape(plane_count, local_columns, width), 'ta...]
    all_to_all x1 -> x0, starting transfers between devices: 7.43 us -> none  [paired_restriction(): lax.all_to_all(projectors.reshape(plane_count, local_columns, width), 'ta...]
    unnamed x24 -> x6, local copies, waits for them, and re-layouts: 3.14 us -> 0.01 us
    broadcast_in_dim x3 -> x0, local copies, waits for them, and re-layouts: 2.07 us -> none  [gather_sums(): copies = jnp.broadcast_to(sums, (devices,) + sums.shape)]
    ppermute x1, waiting for transfers between devices: 1.7 us -> 0.01 us  [paired_restriction(): lax.ppermute(given, 'ta', [(device, device ^ 1) for device in range(plane...]
    squeeze x0 -> x1, local copies, waits for them, and re-layouts: none -> 1.68 us  [paired_restriction(): lax.dynamic_index_in_dim(fine.reshape((chip_count, 2) + fine.shape[1:]),...]
  transfers between devices with their start and end apart: 11 -> 10, of which waited for: 6 -> 4; matrix products, arithmetic and copies ran while one was open for 0% -> 0% of each run, Pallas kernels for 0% -> 0%
where the time goes in v2:
time: 119 us
  blocking collectives  73.7 us (62%)
  waiting for transfers between devices  24.1 us (20%)
  starting transfers between devices  10 us (8%)
  Pallas kernels  8.01 us (7%)
  local copies, waits for them, and re-layouts  1.69 us (1%)
  between operations  1.39 us (1%)
    all_to_all x3, blocking collectives, gather_sums(): return lax.all_to_all(sums, 'ta', 0, 0, tiled=True)  34.7 us
    all_to_all x1, blocking collectives, paired_restriction(): lax.all_to_all(projectors.reshape(chip_count, 2 * local_columns, width),...  23.8 us
    ppermute x3, waiting for transfers between devices, shards(): vectors.append(lax.ppermute(rounded, 'ta', earlier))  23.1 us
    all_to_all x1, blocking collectives, paired_restriction(): lax.all_to_all(summed, 'ta', 0, 0, axis_index_groups=groups, tiled=True)  15.2 us
    pallas_call x7, Pallas kernels, whole_call(): pl.pallas_call(body, out_shape=out_shape, in_specs=specs, out_specs=jax.t...  8.01 us
    ppermute x3, starting transfers between devices, shards(): lax.ppermute(rounded, 'ta', back)  7.93 us
  transfers between devices with their start and end apart: 10, of which 4 were waited for; matrix products, arithmetic and copies ran while one was open for 0% of the time, Pallas kernels for 0%

profile of v2, /device:TPU:0, one launch (start us, length us, event | category | flops | bytes accessed | tf_op | source)
XLA Modules:
  0.0 119.0 jit_solution(11970281080925027168)
XLA Ops:
  0.7 1.7 %dynamic-slice_bitcast_fusion = bf16[8,8,96,128]{3,2,1,0:T(8,128)(2,1)S(1)} fusion(bf16[8,2,8,96,128]{4,3,2,1,0:T(8,128)(2,1)} %bitcast.11, s32[]{:T(128)S(6)} %select_n.12), kind=kLoop, calls=%fused_computation | loop fusion | bytes 3145732 | tf_op jit(solution)/shard_map/jit(dynamic_index_in_dim)/squeeze | solution.py:111
  2.3 0.6 collective-permute-start
  2.9 23.8 %all_to_all.25.proj_ref = bf16[8,16,2304]{2,1,0:T(8,128)(2,1)S(1)} all-to-all(bf16[8,16,2304]{2,1,0:T(8,128)(2,1)S(1)} %bitcast.16), channel_id=1, replica_groups={{0,2,4,6,8,10,12,14},{1,3,5,7,9,11,13,15},{16,18,20,22,24,26,28,30},{17..., dimensions={0} | all-to-all | bytes 1179648 | tf_op jit(solution)/shard_map/all_to_all | solution.py:101
  26.7 3.8 %restrict.1 = f32[8,96,128]{2,1,0:T(8,128)S(1)} custom-call(s32[1]{0:T(128)} %bitcast.1.parity_ref, bf16[8,16,2304]{2,1,0:T(8,128)(2,1)S(1)} %all_to_all.25.proj_ref, bf16[16,8,96,128]{3,2,1,0:T(8,128)(2,1)S(1)} %bitcast.12, bf16[8,8,96,128]{3,2,1,0:T(8,128)(2,1)S(1)} %collective-permute-done.other_ref), custom_call_target="tpu_custom_call" | custom-call | tf_op jit(solution)/shard_map/restrict/pallas_call | solution.py:20
  30.6 15.2 %all_to_all.26.refs_2_ = f32[8,96,128]{2,1,0:T(8,128)S(1)} all-to-all(f32[8,96,128]{2,1,0:T(8,128)S(1)} %restrict.1), channel_id=1, replica_groups={{0,2,4,6,8,10,12,14},{1,3,5,7,9,11,13,15},{16,18,20,22,24,26,28,30},{17..., dimensions={0} | all-to-all | bytes 786432 | tf_op jit(solution)/shard_map/all_to_all | solution.py:123
  45.8 1.0 collective-permute-start.3
  46.8 2.6 %collective-permute-start.1 = (bf16[8,96,128]{2,1,0:T(8,128)(2,1)S(1)}, bf16[8,96,128]{2,1,0:T(8,128)(2,1)S(1)}, u32[]{:S(2)}, u32[]{:S(2)}) collective-permute-start(bf16[8,96,128]{2,1,0:T(8,128)(2,1)S(1)} %convert_element_type.3.refs_3_), channel_id=1, source_target_pairs={{1,0},{2,1},{3,2},{4,3},{5,4},{6,5},{7,6},{0,7},{9,8},{10,9},{11,1... | collective-permute-start | bytes 589832 | tf_op jit(solution)/shard_map/ppermute | solution.py:307
  50.1 5.8 %collective-permute-done.3.refs_6_ = bf16[8,96,128]{2,1,0:T(8,128)(2,1)S(1)} collective-permute-done((bf16[8,96,128]{2,1,0:T(8,128)(2,1)S(1)}, bf16[8,96,128]{2,1,0:T(8,128)(2,1)S(1)}, u32[]{:S(2)}, u32[]{:S(2)}) %collective-permute-start.3) | collective-permute-done | bytes 196640 | tf_op jit(solution)/shard_map/ppermute | solution.py:308
  55.9 1.0 collective-permute-done.2.refs_5_
  56.9 0.8 operator_0.1
  57.8 11.4 %all_to_all.27.refs_0_ = f32[16,8,128]{2,1,0:T(8,128)S(1)} all-to-all(f32[16,8,128]{2,1,0:T(8,128)S(1)} %get-tuple-element.20), channel_id=1, replica_groups=mesh['cfg'=2,'ta'=16] {'ta'}, dimensions={0} | all-to-all | bytes 131072 | tf_op jit(solution)/shard_map/all_to_all | solution.py:277
  69.2 0.2 update_0.1
  69.4 0.3 collective-permute-start.6
  69.6 2.6 %collective-permute-start.4 = (bf16[8,96,128]{2,1,0:T(8,128)(2,1)S(1)}, bf16[8,96,128]{2,1,0:T(8,128)(2,1)S(1)}, u32[]{:S(2)}, u32[]{:S(2)}) collective-permute-start(bf16[8,96,128]{2,1,0:T(8,128)(2,1)S(1)} %get-tuple-element.23.refs_3_), channel_id=1, source_target_pairs={{1,0},{2,1},{3,2},{4,3},{5,4},{6,5},{7,6},{0,7},{9,8},{10,9},{11,1... | collective-permute-start | bytes 589832 | tf_op jit(solution)/shard_map/ppermute | solution.py:307
  72.3 8.6 %collective-permute-done.6.refs_6_ = bf16[8,96,128]{2,1,0:T(8,128)(2,1)S(1)} collective-permute-done((bf16[8,96,128]{2,1,0:T(8,128)(2,1)S(1)}, bf16[8,96,128]{2,1,0:T(8,128)(2,1)S(1)}, u32[]{:S(2)}, u32[]{:S(2)}) %collective-permute-start.6) | collective-permute-done | bytes 196640 | tf_op jit(solution)/shard_map/ppermute | solution.py:308
  80.9 0.8 operator_1.1
  81.8 11.1 %all_to_all.28.refs_0_ = f32[16,8,128]{2,1,0:T(8,128)S(1)} all-to-all(f32[16,8,128]{2,1,0:T(8,128)S(1)} %get-tuple-element.25), channel_id=1, replica_groups=mesh['cfg'=2,'ta'=16] {'ta'}, dimensions={0} | all-to-all | bytes 131072 | tf_op jit(solution)/shard_map/all_to_all | solution.py:277
  92.9 0.3 update_1.1
  93.2 0.3 collective-permute-start.9
  93.5 2.6 %collective-permute-start.7 = (bf16[8,96,128]{2,1,0:T(8,128)(2,1)S(1)}, bf16[8,96,128]{2,1,0:T(8,128)(2,1)S(1)}, u32[]{:S(2)}, u32[]{:S(2)}) collective-permute-start(bf16[8,96,128]{2,1,0:T(8,128)(2,1)S(1)} %get-tuple-element.30.refs_3_), channel_id=1, source_target_pairs={{1,0},{2,1},{3,2},{4,3},{5,4},{6,5},{7,6},{0,7},{9,8},{10,9},{11,1... | collective-permute-start | bytes 589832 | tf_op jit(solution)/shard_map/ppermute | solution.py:307
  96.1 8.6 %collective-permute-done.9.refs_6_ = bf16[8,96,128]{2,1,0:T(8,128)(2,1)S(1)} collective-permute-done((bf16[8,96,128]{2,1,0:T(8,128)(2,1)S(1)}, bf16[8,96,128]{2,1,0:T(8,128)(2,1)S(1)}, u32[]{:S(2)}, u32[]{:S(2)}) %collective-permute-start.9) | collective-permute-done | bytes 196640 | tf_op jit(solution)/shard_map/ppermute | solution.py:308
  104.7 0.9 operator_2.1
  105.6 12.2 %all_to_all.29.refs_0_ = f32[16,16,128]{2,1,0:T(8,128)S(1)} all-to-all(f32[16,16,128]{2,1,0:T(8,128)S(1)} %get-tuple-element.32), channel_id=1, replica_groups=mesh['cfg'=2,'ta'=16] {'ta'}, dimensions={0} | all-to-all | bytes 262144 | tf_op jit(solution)/shard_map/all_to_all | solution.py:277
  117.8 1.2 %update_2.1 = (f32[8,96,128]{2,1,0:T(8,128)}, f32[8,96,128]{2,1,0:T(8,128)}) custom-call(f32[16,16,128]{2,1,0:T(8,128)S(1)} %all_to_all.29.refs_0_, f32[8,96,128]{2,1,0:T(8,128)S(1)} %get-tuple-element.33.refs_1_, f32[8,96,128]{2,1,0:T(8,128)S(1)} %get-tuple-element.29.refs_2_, f32[8,96,128]{2,1,0:T(8,128)S(1)} %get-tuple-element.24.refs_7_.refs_3_, ...), custom_call_target="tpu_custom_call" | custom-call | tf_op jit(solution)/shard_map/update_2/pallas_call | solution.py:20
  (16 shorter events, 0.1 us)
Async XLA Ops:
  0.6 2.3 %copy-start.2 = (bf16[1,128,2304]{2,1,0:T(8,128)(2,1)S(1)}, bf16[1,128,2304]{2,1,0:T(8,128)(2,1)}, u32[]{:S(2)}) copy-start(bf16[1,128,2304]{2,1,0:T(8,128)(2,1)} %param.5) | copy-start | bytes 1769476
  0.7 26.1 %copy-start = (bf16[16,8,2,2,24,128]{5,4,3,2,1,0:T(8,128)(2,1)S(1)}, bf16[16,8,2,2,24,128]{5,4,3,2,1,0:T(8,128)(2,1)}, u32[]{:S(2)}) copy-start(bf16[16,8,2,2,24,128]{5,4,3,2,1,0:T(8,128)(2,1)} %param.4) | copy-start | bytes 9437188
  2.3 24.4 %collective-permute-start = (bf16[8,8,96,128]{3,2,1,0:T(8,128)(2,1)S(1)}, bf16[8,8,96,128]{3,2,1,0:T(8,128)(2,1)S(1)}, u32[]{:S(2)}, u32[]{:S(2)}) collective-permute-start(bf16[8,8,96,128]{3,2,1,0:T(8,128)(2,1)S(1)} %dynamic-slice_bitcast_fusion), channel_id=1, source_target_pairs={{0,1},{1,0},{2,3},{3,2},{4,5},{5,4},{6,7},{7,6},{8,9},{9,8},{10,11... | collective-permute-start | bytes 4718600 | tf_op jit(solution)/shard_map/ppermute | solution.py:114
  30.6 26.4 %copy-start.1 = (bf16[1,8,48,864]{3,2,1,0:T(8,128)(2,1)S(1)}, bf16[1,8,48,864]{3,2,1,0:T(8,128)(2,1)}, u32[]{:S(2)}) copy-start(bf16[1,8,48,864]{3,2,1,0:T(8,128)(2,1)} %param.6) | copy-start | bytes 1990660
  45.8 10.1 %collective-permute-start.3 = (bf16[8,96,128]{2,1,0:T(8,128)(2,1)S(1)}, bf16[8,96,128]{2,1,0:T(8,128)(2,1)S(1)}, u32[]{:S(2)}, u32[]{:S(2)}) collective-permute-start(bf16[8,96,128]{2,1,0:T(8,128)(2,1)S(1)} %convert_element_type.3.refs_3_), channel_id=1, source_target_pairs={{8,0},{9,1},{10,2},{11,3},{12,4},{13,5},{14,6},{15,7},{0,8},{1,9},... | collective-permute-start | bytes 589832 | tf_op jit(solution)/shard_map/ppermute | solution.py:308
  46.8 10.2 %collective-permute-start.2 = (bf16[8,96,128]{2,1,0:T(8,128)(2,1)S(1)}, bf16[8,96,128]{2,1,0:T(8,128)(2,1)S(1)}, u32[]{:S(2)}, u32[]{:S(2)}) collective-permute-start(bf16[8,96,128]{2,1,0:T(8,128)(2,1)S(1)} %convert_element_type.3.refs_3_), channel_id=1, source_target_pairs={{0,1},{1,2},{2,3},{3,4},{4,5},{5,6},{6,7},{7,0},{8,9},{9,10},{10,1... | collective-permute-start | bytes 589832 | tf_op jit(solution)/shard_map/ppermute | solution.py:307
  46.8 10.2 %collective-permute-start.1 = (bf16[8,96,128]{2,1,0:T(8,128)(2,1)S(1)}, bf16[8,96,128]{2,1,0:T(8,128)(2,1)S(1)}, u32[]{:S(2)}, u32[]{:S(2)}) collective-permute-start(bf16[8,96,128]{2,1,0:T(8,128)(2,1)S(1)} %convert_element_type.3.refs_3_), channel_id=1, source_target_pairs={{1,0},{2,1},{3,2},{4,3},{5,4},{6,5},{7,6},{0,7},{9,8},{10,9},{11,1... | collective-permute-start | bytes 589832 | tf_op jit(solution)/shard_map/ppermute | solution.py:307
  69.4 11.5 %collective-permute-start.6 = (bf16[8,96,128]{2,1,0:T(8,128)(2,1)S(1)}, bf16[8,96,128]{2,1,0:T(8,128)(2,1)S(1)}, u32[]{:S(2)}, u32[]{:S(2)}) collective-permute-start(bf16[8,96,128]{2,1,0:T(8,128)(2,1)S(1)} %get-tuple-element.23.refs_3_), channel_id=1, source_target_pairs={{8,0},{9,1},{10,2},{11,3},{12,4},{13,5},{14,6},{15,7},{0,8},{1,9},... | collective-permute-start | bytes 589832 | tf_op jit(solution)/shard_map/ppermute | solution.py:308
  69.6 11.3 %collective-permute-start.5 = (bf16[8,96,128]{2,1,0:T(8,128)(2,1)S(1)}, bf16[8,96,128]{2,1,0:T(8,128)(2,1)S(1)}, u32[]{:S(2)}, u32[]{:S(2)}) collective-permute-start(bf16[8,96,128]{2,1,0:T(8,128)(2,1)S(1)} %get-tuple-element.23.refs_3_), channel_id=1, source_target_pairs={{0,1},{1,2},{2,3},{3,4},{4,5},{5,6},{6,7},{7,0},{8,9},{9,10},{10,1... | collective-permute-start | bytes 589832 | tf_op jit(solution)/shard_map/ppermute | solution.py:307
  69.6 11.3 %collective-permute-start.4 = (bf16[8,96,128]{2,1,0:T(8,128)(2,1)S(1)}, bf16[8,96,128]{2,1,0:T(8,128)(2,1)S(1)}, u32[]{:S(2)}, u32[]{:S(2)}) collective-permute-start(bf16[8,96,128]{2,1,0:T(8,128)(2,1)S(1)} %get-tuple-element.23.refs_3_), channel_id=1, source_target_pairs={{1,0},{2,1},{3,2},{4,3},{5,4},{6,5},{7,6},{0,7},{9,8},{10,9},{11,1... | collective-permute-start | bytes 589832 | tf_op jit(solution)/shard_map/ppermute | solution.py:307
  93.2 11.5 %collective-permute-start.9 = (bf16[8,96,128]{2,1,0:T(8,128)(2,1)S(1)}, bf16[8,96,128]{2,1,0:T(8,128)(2,1)S(1)}, u32[]{:S(2)}, u32[]{:S(2)}) collective-permute-start(bf16[8,96,128]{2,1,0:T(8,128)(2,1)S(1)} %get-tuple-element.30.refs_3_), channel_id=1, source_target_pairs={{8,0},{9,1},{10,2},{11,3},{12,4},{13,5},{14,6},{15,7},{0,8},{1,9},... | collective-permute-start | bytes 589832 | tf_op jit(solution)/shard_map/ppermute | solution.py:308
  93.5 11.3 %collective-permute-start.8 = (bf16[8,96,128]{2,1,0:T(8,128)(2,1)S(1)}, bf16[8,96,128]{2,1,0:T(8,128)(2,1)S(1)}, u32[]{:S(2)}, u32[]{:S(2)}) collective-permute-start(bf16[8,96,128]{2,1,0:T(8,128)(2,1)S(1)} %get-tuple-element.30.refs_3_), channel_id=1, source_target_pairs={{0,1},{1,2},{2,3},{3,4},{4,5},{5,6},{6,7},{7,0},{8,9},{9,10},{10,1... | collective-permute-start | bytes 589832 | tf_op jit(solution)/shard_map/ppermute | solution.py:307
  93.5 11.3 %collective-permute-start.7 = (bf16[8,96,128]{2,1,0:T(8,128)(2,1)S(1)}, bf16[8,96,128]{2,1,0:T(8,128)(2,1)S(1)}, u32[]{:S(2)}, u32[]{:S(2)}) collective-permute-start(bf16[8,96,128]{2,1,0:T(8,128)(2,1)S(1)} %get-tuple-element.30.refs_3_), channel_id=1, source_target_pairs={{1,0},{2,1},{3,2},{4,3},{5,4},{6,5},{7,6},{0,7},{9,8},{10,9},{11,1... | collective-permute-start | bytes 589832 | tf_op jit(solution)/shard_map/ppermute | solution.py:307
